TPU v7x, 32 devices: a whole 2x2x4 slice. The times are simulated.
32 devices in a mesh: gx: 2 (over y), gy: 4 (over x, core), gz: 4 (over z).
Axes of the slice: x: 2, y: 2, z: 4, core: 2. Of those that a mesh axis runs over, the one named last changes fastest.
Arguments:
- loads: float32 [16, 4, 16, 1024], P(None, 'gx', 'gy', 'gz'), may hold values from -60 to 60
- moduli: float32 [8], replicated, may hold values from 0.5 to 4
- material: int32 [4, 16, 1024], P('gx', 'gy', 'gz'), may hold values from 0 to 7
Outputs:
- solution: float32 [16, 4, 16, 1024], P(None, 'gx', 'gy', 'gz')
- residual: float32 [16, 4, 16, 1024], P(None, 'gx', 'gy', 'gz')
All inputs are finite; a program needn't handle non-finite values.
Results may differ from a plain program's by a relative error of at most 0.005.
The roundings to bfloat16 on the way count: a program that leaves them out, or rounds other values in their place, can miss the bound.
Values may be sent and summed in bfloat16 or wider, within the bound.
A program may use at most 64 MiB of HBM per device.

v0:
```python
import functools
import itertools

import jax
import jax.numpy as jnp
import numpy as np
from jax import lax
from jax.experimental import pallas as pl
from jax.experimental.pallas import tpu as pltpu
from jax.sharding import PartitionSpec as P

SIGMA = 0.25
AXES = ("gx", "gy", "gz")
HIGH = lax.Precision.HIGHEST
F32 = jnp.float32
BF16 = jnp.bfloat16
LANES = 128
DIRECT_LIMIT = 32


def stiffness_values():
    mass = (1.0 / 3.0, 1.0 / 6.0)
    stiff = (1.0, -1.0)
    values = []
    for differing in range(4):
        bits = [1 if dim < differing else 0 for dim in range(3)]
        total = 0.0
        for dim in range(3):
            factor = 1.0
            for other in range(3):
                factor *= stiff[bits[other]] if other == dim else mass[bits[other]]
            total += factor
        values.append(float(np.asarray(total, np.float32).astype(jnp.bfloat16).astype(np.float32)))
    return values


def dot(left, right, left_dim, right_dim, precision=HIGH):
    return lax.dot_general(
        left, right, (((left_dim,), (right_dim,)), ((), ())), precision=precision, preferred_element_type=F32
    )


def pack(matrix):
    rows, cols = matrix.shape
    wide = jnp.concatenate([matrix, jnp.zeros((rows, LANES - cols), F32)], axis=1)
    pieces = [
        jnp.sum(pltpu.roll(wide[start : start + 8], 0, 1, stride=cols, stride_axis=0), axis=0, keepdims=True)
        for start in range(0, rows, 8)
    ]
    return jnp.concatenate(pieces, axis=0)


def unpack(tile, cols):
    rows = tile.shape[0]
    tall = jnp.concatenate([tile, jnp.zeros((8 - rows, LANES), F32)], axis=0)
    turned = [tall] + [pltpu.roll(tall, LANES - cols * group, 1) for group in range(1, 8)]
    return jnp.concatenate(
        [turned[group][row : row + 1] for row in range(rows) for group in range(8)], axis=0
    )[:, 0:cols]


def eliminate(matrix, rhs):
    size = matrix.shape[0]
    both = jnp.concatenate([matrix, rhs], axis=1)
    rows = lax.broadcasted_iota(jnp.int32, both.shape, 0)
    for step in range(0, size, 2):
        top, low = both[step : step + 1, :], both[step + 1 : step + 2, :]
        left, right = both[:, step : step + 1], both[:, step + 1 : step + 2]
        first, mixed, second = top[:, step : step + 1], top[:, step + 1 : step + 2], low[:, step + 1 : step + 2]
        ratio = mixed / first
        low_new = (low - ratio * top) / (second - ratio * mixed)
        top_new = top / first - ratio * low_new
        rest = both - left * top_new - right * low_new
        both = jnp.where(rows == step, top_new, jnp.where(rows == step + 1, low_new, rest))
    return both[:, size:]


def kernel_body(sizes, phases, stiff, moduli_ref, loads_ref, mat_ref, sol_ref, res_ref,
                stack, padded, padded_im, mats_rx, ends, ends_rx, ends_im, ends_im_rx, field, wt, wtr, stack2,
                shares_rr, shares_im, shares_last, halo_send, halo_recv, sum_send, sum_recv,
                out_stage, local_sems, vouch_sem):
    cols, nx, ny, nz = loads_ref.shape
    mats = moduli_ref.shape[0]
    me = [lax.axis_index(axis) for axis in AXES]
    k_self, k_edge, k_far = stiff[0], stiff[1], stiff[2]
    assert k_edge == 0.0 and stiff[2] == stiff[3]
    xs, ys = range(nx + 2), range(ny + 2)
    shares_of = (shares_rr, shares_im, shares_last)
    own = list(itertools.product(range(nx), range(ny)))

    directions = [
        d for d in itertools.product((-1, 0, 1), repeat=3)
        if any(d) and all(step == 0 or sizes[i] > 1 for i, step in enumerate(d))
    ]

    def exists(direction):
        good = None
        for i, step in enumerate(direction):
            if step:
                here = (me[i] > 0) if step < 0 else (me[i] < sizes[i] - 1)
                good = here if good is None else jnp.logical_and(good, here)
        return good

    def target(direction):
        return {axis: me[i] + direction[i] for i, axis in enumerate(AXES)}

    def place(direction):
        return 1 - direction[0], 1 - direction[1]

    def halo_copies(round_, number):
        direction = dx, dy, dz = directions[number]
        core, source, edge = ((padded, ends, ends_rx), (padded_im, ends_im, ends_im_rx))[round_]
        pairs = []
        if dz == 0:
            src_x = {0: pl.ds(1, nx), 1: pl.ds(nx, 1), -1: pl.ds(1, 1)}[dx]
            dst_x = {0: pl.ds(1, nx), 1: pl.ds(0, 1), -1: pl.ds(nx + 1, 1)}[dx]
            src_y = {0: pl.ds(1, ny), 1: pl.ds(ny, 1), -1: pl.ds(1, 1)}[dy]
            dst_y = {0: pl.ds(1, ny), 1: pl.ds(0, 1), -1: pl.ds(ny + 1, 1)}[dy]
            pairs.append((core.at[src_x, src_y], core.at[dst_x, dst_y]))
            if round_ == 0:
                pairs.append((mats_rx.at[1, 1], mats_rx.at[place(direction)]))
        else:
            pairs.append((source.at[1 if dz > 0 else 0], edge.at[(*place(direction), 0 if dz > 0 else 1)]))
        return [
            pltpu.make_async_remote_copy(
                src_ref=src, dst_ref=dst, send_sem=halo_send.at[round_ + 2 * i, number],
                recv_sem=halo_recv.at[round_ + 2 * i, number],
                device_id=target(direction), device_id_type=pl.DeviceIdType.MESH,
            )
            for i, (src, dst) in enumerate(pairs)
        ]

    def halo_each(round_, act, incoming=False):
        for number, direction in enumerate(directions):
            @pl.when(exists(tuple(-step for step in direction) if incoming else direction))
            def _():
                for copy in halo_copies(round_, number):
                    act(copy)

    def halo_start(round_):
        halo_each(round_, lambda copy: copy.start())

    def halo_arrive(round_):
        halo_each(round_, lambda copy: copy.wait_recv(), True)

    def halo_left(round_):
        halo_each(round_, lambda copy: copy.wait_send())

    def each(count, body):
        if count <= 8:
            for k in range(1, count):
                body(k, 0)
        else:
            lax.fori_loop(1, count, body, 0)

    def group_of(axes):
        count, index = 1, 0
        for axis in axes:
            i = AXES.index(axis)
            count *= sizes[i]
            index = index * sizes[i] + me[i]
        return count, index

    def peer_id(axes, peer):
        coords = {axis: me[i] for i, axis in enumerate(AXES)}
        for axis in reversed(axes):
            size = sizes[AXES.index(axis)]
            coords[axis] = lax.rem(peer, size)
            peer = lax.div(peer, size)
        return coords

    offsets = []
    total_slots = 0
    for axes in phases:
        offsets.append(total_slots)
        total_slots += group_of(axes)[0]

    def fetch(x, y):
        return pltpu.make_async_copy(
            loads_ref.at[:, x, y, :], stack.at[x, y, pl.ds(0, cols), :], local_sems.at[0, x * ny + y]
        )

    def put(which, ref, x, y):
        return pltpu.make_async_copy(
            out_stage.at[which, x, y], ref.at[:, x, y, :], local_sems.at[1 + which, x * ny + y]
        )

    for x, y in own:
        fetch(x, y).start()

    for x in xs:
        for y in ys:
            if not (1 <= x <= nx and 1 <= y <= ny):
                padded[x, y] = jnp.zeros(padded.shape[2:], BF16)
                padded_im[x, y] = jnp.zeros(padded_im.shape[2:], BF16)
    for bx, by in itertools.product(range(3), repeat=2):
        mats_rx[bx, by] = jnp.zeros(mats_rx.shape[2:], F32)
        for side in range(2):
            ends_rx[bx, by, side] = jnp.zeros(ends_rx.shape[3:], BF16)
            ends_im_rx[bx, by, side] = jnp.zeros(ends_im_rx.shape[3:], BF16)

    barrier = pltpu.get_barrier_semaphore()
    expected = 0
    if len(phases) == 1:
        flat = sizes[0] * sizes[1]
        spot = me[0] * sizes[1] + me[1]
        for dz in (-1, 0, 1):
            good = True if dz == 0 else exists((0, 0, dz))

            def greet(k, carry, dz=dz):
                there = lax.rem(spot + k, flat)
                pl.semaphore_signal(
                    barrier, inc=1, device_id_type=pl.DeviceIdType.MESH,
                    device_id={"gx": lax.div(there, sizes[1]), "gy": lax.rem(there, sizes[1]), "gz": me[2] + dz},
                )
                return carry

            if dz == 0:
                each(flat, greet)
                expected = expected + flat - 1
            elif sizes[2] > 1:
                @pl.when(good)
                def _():
                    greet(0, 0)
                    each(flat, greet)
                expected = expected + jnp.where(good, flat, 0)
    else:
        for axes in phases:
            count, index = group_of(axes)

            def greet(k, carry, axes=axes, count=count, index=index):
                pl.semaphore_signal(barrier, inc=1, device_id=peer_id(axes, lax.rem(index + k, count)),
                                    device_id_type=pl.DeviceIdType.MESH)
                return carry

            each(count, greet)
            expected = expected + count - 1
        for direction in directions:
            good = exists(direction)

            @pl.when(good)
            def _():
                pl.semaphore_signal(barrier, inc=1, device_id=target(direction),
                                    device_id_type=pl.DeviceIdType.MESH)
            expected = expected + jnp.where(good, 1, 0)

    vouches = max(sizes[2] - 2, 0) if len(phases) == 1 else 0

    def vouch(round_):
        for dz in (-1, 1):
            @pl.when(exists((0, 0, dz)))
            def _():
                pl.semaphore_signal(vouch_sem.at[round_, 0 if dz > 0 else 1], inc=1, device_id=target((0, 0, dz)),
                                    device_id_type=pl.DeviceIdType.MESH)

    def vouched(round_):
        for dz in (-1, 1):
            @pl.when(exists((0, 0, dz)))
            def _():
                pl.semaphore_wait(vouch_sem.at[round_, 1 if dz > 0 else 0], 1)

    lane = lax.broadcasted_iota(jnp.int32, (1, LANES), 1)
    firsts = lasts = jnp.zeros((2 * cols, LANES), F32)
    for x in range(nx):
        mats_rx[1, 1, x * ny : (x + 1) * ny, :] = (mat_ref[x] + 1).astype(F32)
    for x, y in own:
        fetch(x, y).wait()
        values = stack[x, y, 0:cols, :]
        padded[x + 1, y + 1] = values.astype(BF16)
        row = x * ny + y
        ids = jnp.broadcast_to(mats_rx[1, 1, row : row + 1, :], (cols, nz))
        column = jnp.concatenate([values, ids], axis=0)
        firsts = jnp.where(lane == row, column[:, 0:1], firsts)
        lasts = jnp.where(lane == row, column[:, nz - 1 : nz], lasts)
    ends[0] = firsts.astype(BF16)
    ends[1] = lasts.astype(BF16)
    pl.semaphore_wait(barrier, expected)
    halo_start(0)
    if vouches:
        vouch(0)

    def block_of(x, y):
        bx, lx = (0, nx - 1) if x == 0 else (2, 0) if x == nx + 1 else (1, x - 1)
        by, ly = (0, ny - 1) if y == 0 else (2, 0) if y == ny + 1 else (1, y - 1)
        return bx, by, lx * ny + ly

    def merged(edge, x, y):
        bx, by, row = block_of(x, y)
        left, right = edge[bx, by, 0].astype(F32), edge[bx, by, 1].astype(F32)
        return jnp.where(lane == 0, right[:, row : row + 1],
                         jnp.where(lane == LANES - 1, left[:, row : row + 1], 0.0))

    def gram(left, right):
        total = None
        for x, y in own:
            part = dot(left(x, y), right(x, y), 1, 1)
            total = part if total is None else total + part
        return total

    def sum_copy(round_, number, k):
        axes = phases[number]
        count, index = group_of(axes)
        slot = offsets[number] + index
        return pltpu.make_async_remote_copy(
            src_ref=shares_of[round_].at[slot], dst_ref=shares_of[round_].at[slot],
            send_sem=sum_send.at[round_, offsets[number] + k], recv_sem=sum_recv.at[round_, offsets[number] + k],
            device_id=peer_id(axes, lax.rem(index + k, count)), device_id_type=pl.DeviceIdType.MESH,
        )

    def sum_arrival(round_, number, k):
        axes = phases[number]
        count, index = group_of(axes)
        source = lax.rem(index + count - k, count)
        slot = offsets[number] + source
        return pltpu.make_async_remote_copy(
            src_ref=shares_of[round_].at[slot], dst_ref=shares_of[round_].at[slot],
            send_sem=sum_send.at[round_, offsets[number] + k], recv_sem=sum_recv.at[round_, offsets[number] + k],
            device_id=peer_id(axes, lax.rem(index + k, count)), device_id_type=pl.DeviceIdType.MESH,
        )

    def sum_start(round_, number, tile):
        count, index = group_of(phases[number])
        shares_of[round_][offsets[number] + index] = tile

        def send(k, carry):
            sum_copy(round_, number, k).start()
            return carry

        each(count, send)

    def sum_finish(round_, number):
        count, _ = group_of(phases[number])

        def receive(k, carry):
            sum_arrival(round_, number, k).wait_recv()
            return carry

        each(count, receive)
        tile = shares_of[round_][offsets[number]]
        for peer in range(1, count):
            tile = tile + shares_of[round_][offsets[number] + peer]
        return tile

    def sum_turn(round_):
        for number in range(1, len(phases)):
            sum_start(round_, number, sum_finish(round_, number - 1))

    def sum_rest(round_):
        return unpack(sum_finish(round_, len(phases) - 1), cols)

    def sum_left(round_):
        for number, axes in enumerate(phases):
            def drain(k, carry, number=number):
                sum_copy(round_, number, k).wait_send()
                return carry

            each(group_of(axes)[0], drain)

    def loads_at(x, y):
        return stack[x, y, 0:cols, :]

    def image_at(x, y):
        return stack[x, y, cols:, :]

    def loads_at2(x, y):
        return stack2[x, y, 0:cols, :]

    def image_at2(x, y):
        return stack2[x, y, cols:, :]

    load_part = pack(gram(loads_at, loads_at))
    for round_ in range(1, vouches):
        vouched(round_ - 1)
        vouch(round_)
    halo_arrive(0)
    full = nz + LANES
    moduli = {}
    for x in xs:
        for y in ys:
            tail = merged(ends_rx, x, y)
            field[x, y] = jnp.concatenate([padded[x, y].astype(F32), tail[0:cols]], axis=1)
            bx, by, row = block_of(x, y)
            ids = jnp.concatenate([
                jnp.broadcast_to(mats_rx[bx, by, row : row + 1, :], (8, nz)), tail[cols : cols + 8]
            ], axis=1)
            modulus = jnp.zeros_like(ids)
            for number in range(mats):
                modulus = modulus + jnp.where(ids == float(number + 1), moduli_ref[number], 0.0)
            moduli[x, y] = modulus
    for x in range(nx + 1):
        for y in range(ny + 1):
            total = (moduli[x, y] + moduli[x, y + 1]) + (moduli[x + 1, y] + moduli[x + 1, y + 1])
            weight = 0.125 * (total + pltpu.roll(total, full - 1, 1))
            wt[x, y] = weight
            wtr[x, y] = pltpu.roll(weight, 1, 1)

    if vouches:
        vouched(vouches - 1)
    sum_start(0, 0, load_part)
    sum_turn(0)

    def double(tile):
        return jnp.concatenate([tile, tile], axis=0)

    def operate(direction_of, write):
        for x in range(nx):
            for y in range(ny):
                here = field[x + 1, y + 1]
                ahead = behind = flat = None
                w_ahead = w_behind = None
                for ex in (x, x + 1):
                    for ey in (y, y + 1):
                        corner_sum = (field[ex, ey] + field[ex, ey + 1]) + (field[ex + 1, ey] + field[ex + 1, ey + 1])
                        after, before = wt[ex, ey], wtr[ex, ey]
                        opposite = field[2 * ex - x, 2 * ey - y][:, 0:nz]
                        one = double(before) * corner_sum
                        two = double(after) * corner_sum
                        three = double((before + after)[:, 0:nz]) * opposite
                        ahead = one if ahead is None else ahead + one
                        behind = two if behind is None else behind + two
                        flat = three if flat is None else flat + three
                        w_ahead = before if w_ahead is None else w_ahead + before
                        w_behind = after if w_behind is None else w_behind + after
                ahead = ahead - double(w_ahead) * here
                behind = behind - double(w_behind) * here
                around = pltpu.roll(ahead, full - 1, 1)[:, 0:nz] + pltpu.roll(behind, 1, 1)[:, 0:nz] + flat
                centre = double((w_ahead + w_behind)[:, 0:nz]) * here[:, 0:nz]
                write(x, y, SIGMA * direction_of(x, y) + (k_far * around + k_self * centre))

    image_firsts = jnp.zeros((cols, LANES), F32)
    image_ends = [image_firsts, image_firsts]

    def write_first(x, y, image):
        stack[x, y, cols:, :] = image
        padded_im[x + 1, y + 1] = image.astype(BF16)
        row = x * ny + y
        image_ends[0] = jnp.where(lane == row, image[:, 0:1], image_ends[0])
        image_ends[1] = jnp.where(lane == row, image[:, nz - 1 : nz], image_ends[1])

    operate(loads_at, write_first)
    ends_im[0] = image_ends[0].astype(BF16)
    ends_im[1] = image_ends[1].astype(BF16)
    cross_part = gram(image_at, lambda x, y: stack[x, y])
    sum_start(1, 0, jnp.concatenate([pack(cross_part[:, 0:cols]), pack(cross_part[:, cols:])], axis=0))
    halo_start(1)
    square = sum_rest(0)
    sum_turn(1)
    row_id = lax.broadcasted_iota(jnp.int32, (cols, cols), 0)
    col_id = lax.broadcasted_iota(jnp.int32, (cols, cols), 1)
    eye = jnp.where(row_id == col_id, 1.0, 0.0)
    inverse = eliminate(square, eye)
    table = sum_rest(1)

    cross, quad = table[0:cols], table[cols:]
    alpha = eliminate(0.5 * (cross + cross.T), square)
    updated = square + dot(alpha, dot(quad, alpha, 1, 0) - cross, 0, 0) - dot(cross, alpha, 0, 0)
    beta = dot(inverse, updated, 1, 0)
    alpha_t = alpha.T
    mix = jnp.concatenate([(eye + beta).T, -alpha_t], axis=1)
    mix_hi = mix.astype(BF16)
    mix_lo = (mix - mix_hi.astype(F32)).astype(BF16)
    mix_both = jnp.concatenate([mix_hi, mix_lo], axis=0)

    halo_arrive(1)
    for x in xs:
        for y in ys:
            inner = 1 <= x <= nx and 1 <= y <= ny
            tail_l = merged(ends_rx, x, y)[0:cols].astype(BF16)
            tail_i = merged(ends_im_rx, x, y).astype(BF16)
            if inner:
                near = jnp.concatenate([tail_l, tail_i], axis=0)
            else:
                near = jnp.concatenate([
                    jnp.concatenate([padded[x, y], tail_l], axis=1),
                    jnp.concatenate([padded_im[x, y], tail_i], axis=1),
                ], axis=0)
            twice = dot(mix_both, near, 1, 0, None)
            mixed = twice[0:cols] + twice[cols:]
            if inner:
                direction = dot(mix, stack[x - 1, y - 1], 1, 0)
                stack2[x - 1, y - 1, 0:cols, :] = direction
                mixed = jnp.concatenate([direction, mixed], axis=1)
            field[x, y] = mixed.astype(BF16).astype(F32)

    def write_second(x, y, image):
        stack2[x, y, cols:, :] = image

    operate(loads_at2, write_second)
    sum_start(2, 0, pack(gram(image_at2, loads_at2)))
    for x, y in own:
        out_stage[0, x, y] = dot(alpha_t, stack[x, y, 0:cols, :], 1, 0)
        out_stage[1, x, y] = stack[x, y, 0:cols, :] - dot(alpha_t, stack[x, y, cols:, :], 1, 0)
    halo_left(0)
    halo_left(1)
    sum_left(0)
    sum_left(1)
    sum_turn(2)
    cross2 = sum_rest(2)
    alpha2_t = eliminate(0.5 * (cross2 + cross2.T), updated).T
    for x, y in own:
        out_stage[0, x, y] = out_stage[0, x, y] + dot(alpha2_t, stack2[x, y, 0:cols, :], 1, 0)
        put(0, sol_ref, x, y).start()
        out_stage[1, x, y] = out_stage[1, x, y] - dot(alpha2_t, stack2[x, y, cols:, :], 1, 0)
        put(1, res_ref, x, y).start()
    sum_left(2)
    for x, y in own:
        put(0, sol_ref, x, y).wait()
        put(1, res_ref, x, y).wait()


def on_device(sizes, loads, moduli, material):
    cols, nx, ny, nz = loads.shape
    count = int(np.prod(sizes))
    phases = (AXES,) if count <= DIRECT_LIMIT else (("gx", "gy"), ("gz",))
    slots = sum(int(np.prod([sizes[AXES.index(a)] for a in axes])) for axes in phases)
    body = functools.partial(kernel_body, sizes, phases, stiffness_values())
    out = pltpu.VMEM((cols, nx, ny, nz), F32)
    vmem = pl.BlockSpec(memory_space=pltpu.VMEM)
    anywhere = pl.BlockSpec(memory_space=pl.ANY)
    full = nz + LANES
    return pl.pallas_call(
        body,
        out_shape=(out, out),
        in_specs=[pl.BlockSpec(memory_space=pltpu.SMEM), anywhere, vmem],
        out_specs=(anywhere, anywhere),
        scratch_shapes=[
            pltpu.VMEM((nx, ny, 2 * cols, nz), F32),
            pltpu.VMEM((nx + 2, ny + 2, cols, nz), BF16),
            pltpu.VMEM((nx + 2, ny + 2, cols, nz), BF16),
            pltpu.VMEM((3, 3, nx * ny, nz), F32),
            pltpu.VMEM((2, 2 * cols, LANES), BF16),
            pltpu.VMEM((3, 3, 2, 2 * cols, LANES), BF16),
            pltpu.VMEM((2, cols, LANES), BF16),
            pltpu.VMEM((3, 3, 2, cols, LANES), BF16),
            pltpu.VMEM((nx + 2, ny + 2, cols, full), F32),
            pltpu.VMEM((nx + 1, ny + 1, 8, full), F32),
            pltpu.VMEM((nx + 1, ny + 1, 8, full), F32),
            pltpu.VMEM((nx, ny, 2 * cols, nz), F32),
            pltpu.VMEM((slots, cols * cols // LANES, LANES), F32),
            pltpu.VMEM((slots, 2 * cols * cols // LANES, LANES), F32),
            pltpu.VMEM((slots, cols * cols // LANES, LANES), F32),
            pltpu.SemaphoreType.DMA((3, 26)),
            pltpu.SemaphoreType.DMA((3, 26)),
            pltpu.SemaphoreType.DMA((3, slots)),
            pltpu.SemaphoreType.DMA((3, slots)),
            pltpu.VMEM((2, nx, ny, cols, nz), F32),
            pltpu.SemaphoreType.DMA((3, nx * ny)),
            pltpu.SemaphoreType.REGULAR((max(sizes[2], 2), 2)),
        ],
        compiler_params=pltpu.CompilerParams(collective_id=0, has_side_effects=True),
    )(moduli, loads, material)


def solution(mesh):
    sizes = tuple(mesh.shape[axis] for axis in AXES)
    in_specs = (P(None, "gx", "gy", "gz"), P(), P("gx", "gy", "gz"))
    out_specs = (P(None, "gx", "gy", "gz"), P(None, "gx", "gy", "gz"))
    return jax.shard_map(
        functools.partial(on_device, sizes), mesh=mesh, in_specs=in_specs, out_specs=out_specs, check_vma=False
    )
```

profile of v0, /device:TPU:0, one launch (start us, length us, event | category | flops | bytes accessed | tf_op | source)
XLA Modules:
  0.0 35.0 jit_solution(17384715966097938411)
XLA Ops:
  0.6 33.1 %shard_map.50 = (f32[16,2,4,256]{3,2,1,0:T(4,128)S(1)}, f32[16,2,4,256]{3,2,1,0:T(4,128)S(1)}) custom-call(f32[8]{0:T(128)} %moduli_ref.1, f32[16,2,4,256]{3,2,1,0:T(4,128)} %loads_ref.1, s32[2,4,256]{2,1,0:T(4,128)} %mat_ref.1), custom_call_target="tpu_custom_call" | custom-call | tf_op jit(solution)/shard_map/pallas_call | solution.py:521
  33.7 0.7 %copy.7 = f32[16,2,4,256]{3,2,1,0:T(4,128)} copy(f32[16,2,4,256]{3,2,1,0:T(4,128)S(1)} %get-tuple-element.2) | data formatting | bytes 262144
  34.4 0.7 %copy.8 = f32[16,2,4,256]{3,2,1,0:T(4,128)} copy(f32[16,2,4,256]{3,2,1,0:T(4,128)S(1)} %get-tuple-element.3) | data formatting | bytes 262144
where the time goes:
time: 35.3 us; the launch traced here: 35 us
  Pallas kernels  33.1 us (94%)
  local copies, waits for them, and re-layouts  1.31 us (4%)
  between operations  0.64 us (2%)
    pallas_call x1, Pallas kernels, on_device(): pl.pallas_call(body, out_shape=(out, out), in_specs=[pl.BlockSpec(memory_...  33.1 us
    unnamed x2, local copies, waits for them, and re-layouts  1.31 us

commit v1 on v0

v1 whole, which is shorter than its diff:
```python
import functools
import itertools

import jax
import jax.numpy as jnp
import numpy as np
from jax import lax
from jax.experimental import pallas as pl
from jax.experimental.pallas import tpu as pltpu
from jax.sharding import PartitionSpec as P

SIGMA = 0.25
AXES = ("gx", "gy", "gz")
HIGH = lax.Precision.HIGHEST
F32 = jnp.float32
BF16 = jnp.bfloat16
LANES = 128
DIRECT_LIMIT = 32
IDS = 64


def stiffness_values():
    mass = (1.0 / 3.0, 1.0 / 6.0)
    stiff = (1.0, -1.0)
    values = []
    for differing in range(4):
        bits = [1 if dim < differing else 0 for dim in range(3)]
        total = 0.0
        for dim in range(3):
            factor = 1.0
            for other in range(3):
                factor *= stiff[bits[other]] if other == dim else mass[bits[other]]
            total += factor
        values.append(float(np.asarray(total, np.float32).astype(jnp.bfloat16).astype(np.float32)))
    return values


def dot(left, right, left_dim, right_dim, precision=HIGH):
    return lax.dot_general(
        left, right, (((left_dim,), (right_dim,)), ((), ())), precision=precision, preferred_element_type=F32
    )


def pack(matrix):
    rows, cols = matrix.shape
    wide = jnp.concatenate([matrix, jnp.zeros((rows, LANES - cols), F32)], axis=1)
    pieces = [
        jnp.sum(pltpu.roll(wide[start : start + 8], 0, 1, stride=cols, stride_axis=0), axis=0, keepdims=True)
        for start in range(0, rows, 8)
    ]
    return jnp.concatenate(pieces, axis=0)


def unpack(tile, cols):
    rows = tile.shape[0]
    tall = jnp.concatenate([tile, jnp.zeros((8 - rows, LANES), F32)], axis=0)
    turned = [tall] + [pltpu.roll(tall, LANES - cols * group, 1) for group in range(1, 8)]
    return jnp.concatenate(
        [turned[group][row : row + 1] for row in range(rows) for group in range(8)], axis=0
    )[:, 0:cols]


def solve(matrix, rhs):
    size = matrix.shape[0]
    wide = jnp.concatenate([rhs, jnp.zeros((size, LANES - rhs.shape[1]), F32)], axis=1)
    left = [jnp.broadcast_to(matrix[:, i : i + 1], (size, LANES)) for i in range(size)]
    right = [wide[i : i + 1, :] for i in range(size)]
    start = 0
    for step in range(size):
        if step == size // 2 and step % 8 == 0:
            left = [row[step:, :] for row in left]
            start = step
        at = step - start
        scale = 1.0 / left[step][at : at + 1, :]
        pivot, pivot_right = left[step] * scale, right[step] * scale
        for i in range(size):
            if i != step:
                factor = left[i][at : at + 1, :]
                left[i] = left[i] - factor * pivot
                right[i] = right[i] - factor * pivot_right
        left[step], right[step] = pivot, pivot_right
    return jnp.concatenate(right, axis=0)[:, 0 : rhs.shape[1]]


def tree_sum(terms):
    while len(terms) > 1:
        terms = [a + b for a, b in zip(terms[0::2], terms[1::2])] + terms[len(terms) & ~1 :]
    return terms[0]


def main_body(sizes, plans, stiff, moduli_hbm, loads_ref, mat_hbm, base_ref, pair_ref, coef_ref,
              stack, padded, padded_im, mats_rx, ends, ends_rx, ends_im, ends_im_rx, field, wt, wtr,
              shares_table, shares_last, moduli_ref, mat_ref, credit,
              halo_send, halo_recv, sum_send, sum_recv, local_sems, vouch_sem):
    cols, nx, ny, nz = loads_ref.shape
    mats = moduli_ref.shape[0]
    me = [lax.axis_index(axis) for axis in AXES]
    k_self, k_edge, k_far = stiff[0], stiff[1], stiff[2]
    assert k_edge == 0.0 and stiff[2] == stiff[3]
    assert 2 * nx * ny <= IDS and (nx * ny * nz) % (cols * LANES) == 0 and nz % LANES == 0
    xs, ys = range(nx + 2), range(ny + 2)
    shares_of = (shares_table, shares_last)
    own = list(itertools.product(range(nx), range(ny)))

    directions = [
        d for d in itertools.product((-1, 0, 1), repeat=3)
        if any(d) and all(step == 0 or sizes[i] > 1 for i, step in enumerate(d))
    ]
    directions.sort(key=lambda d: -sum(abs(step) for step in d))

    def exists(direction):
        good = None
        for i, step in enumerate(direction):
            if step:
                here = (me[i] > 0) if step < 0 else (me[i] < sizes[i] - 1)
                good = here if good is None else jnp.logical_and(good, here)
        return good

    def target(direction):
        return {axis: me[i] + direction[i] for i, axis in enumerate(AXES)}

    def place(direction):
        return 1 - direction[0], 1 - direction[1]

    def halo_start(round_):
        core, source, edge = ((padded, ends, ends_rx), (padded_im, ends_im, ends_im_rx))[round_]
        for direction in directions:
            dx, dy, dz = direction
            pairs = []
            if dz == 0:
                src_x = {0: pl.ds(1, nx), 1: pl.ds(nx, 1), -1: pl.ds(1, 1)}[dx]
                dst_x = {0: pl.ds(1, nx), 1: pl.ds(0, 1), -1: pl.ds(nx + 1, 1)}[dx]
                src_y = {0: pl.ds(1, ny), 1: pl.ds(ny, 1), -1: pl.ds(1, 1)}[dy]
                dst_y = {0: pl.ds(1, ny), 1: pl.ds(0, 1), -1: pl.ds(ny + 1, 1)}[dy]
                pairs.append((core.at[src_x, src_y], core.at[dst_x, dst_y]))
                if round_ == 0:
                    pairs.append((mats_rx.at[1, 1], mats_rx.at[place(direction)]))
            else:
                pairs.append((source.at[1 if dz > 0 else 0], edge.at[(*place(direction), 0 if dz > 0 else 1)]))

            @pl.when(exists(direction))
            def _():
                for src, dst in pairs:
                    pltpu.make_async_remote_copy(
                        src_ref=src, dst_ref=dst, send_sem=halo_send.at[round_], recv_sem=halo_recv.at[round_],
                        device_id=target(direction), device_id_type=pl.DeviceIdType.MESH,
                    ).start()

    def halo_wait(round_, sem):
        numbers = [
            ((me[i] > 0).astype(jnp.int32) + (me[i] < sizes[i] - 1).astype(jnp.int32)) for i in range(3)
        ]
        choices = [(0,) if size == 1 else (1,) if size == 2 else (1, 2) for size in sizes]
        per = nz // LANES
        for cx, cy, cz in itertools.product(*choices):
            total = per * (cx * ny + cy * nx + cx * cy) + cz * (1 + cx) * (1 + cy)
            if round_ == 0:
                total += (cx + cy + cx * cy) * (nx * ny * nz // (cols * LANES))
            if total:
                tests = [numbers[i] == c for i, c in enumerate((cx, cy, cz)) if len(choices[i]) > 1]

                def take():
                    part = credit.at[pl.ds(0, total)]
                    pltpu.make_async_copy(part, part, sem).wait()

                if tests:
                    pl.when(functools.reduce(jnp.logical_and, tests))(take)
                else:
                    take()

    def each(count, body):
        if count <= 8:
            for k in range(1, count):
                body(k, 0)
        else:
            lax.fori_loop(1, count, body, 0)

    def group_of(axes):
        count, index = 1, 0
        for axis in axes:
            i = AXES.index(axis)
            count *= sizes[i]
            index = index * sizes[i] + me[i]
        return count, index

    def peer_id(axes, peer):
        coords = {axis: me[i] for i, axis in enumerate(AXES)}
        for axis in reversed(axes):
            size = sizes[AXES.index(axis)]
            coords[axis] = lax.rem(peer, size)
            peer = lax.div(peer, size)
        return coords

    def offset_of(round_, number):
        return sum(group_of(axes)[0] for axes in plans[round_][:number])

    direct = (AXES,) in plans

    for bx, by in itertools.product(range(3), repeat=2):
        for side in range(2):
            ends_rx[bx, by, side] = jnp.zeros(ends_rx.shape[3:], BF16)
            ends_im_rx[bx, by, side] = jnp.zeros(ends_im_rx.shape[3:], BF16)
        if (bx, by) != (1, 1):
            mats_rx[bx, by] = jnp.zeros(mats_rx.shape[2:], BF16)
    for x in xs:
        for y in ys:
            if not (1 <= x <= nx and 1 <= y <= ny):
                padded[x, y] = jnp.zeros(padded.shape[2:], BF16)
                padded_im[x, y] = jnp.zeros(padded_im.shape[2:], BF16)

    barrier = pltpu.get_barrier_semaphore()
    expected = 0
    if direct:
        flat = sizes[0] * sizes[1]
        spot = me[0] * sizes[1] + me[1]
        for dz in (-1, 0, 1):
            good = True if dz == 0 else exists((0, 0, dz))

            def greet(k, carry, dz=dz):
                there = lax.rem(spot + k, flat)
                pl.semaphore_signal(
                    barrier, inc=1, device_id_type=pl.DeviceIdType.MESH,
                    device_id={"gx": lax.div(there, sizes[1]), "gy": lax.rem(there, sizes[1]), "gz": me[2] + dz},
                )
                return carry

            if dz == 0:
                each(flat, greet)
                expected = expected + flat - 1
            elif sizes[2] > 1:
                @pl.when(good)
                def _():
                    greet(0, 0)
                    each(flat, greet)
                expected = expected + jnp.where(good, flat, 0)
    else:
        for axes in plans[0]:
            count, index = group_of(axes)

            def greet(k, carry, axes=axes, count=count, index=index):
                pl.semaphore_signal(barrier, inc=1, device_id=peer_id(axes, lax.rem(index + k, count)),
                                    device_id_type=pl.DeviceIdType.MESH)
                return carry

            each(count, greet)
            expected = expected + count - 1
        for direction in directions:
            good = exists(direction)

            @pl.when(good)
            def _():
                pl.semaphore_signal(barrier, inc=1, device_id=target(direction),
                                    device_id_type=pl.DeviceIdType.MESH)
            expected = expected + jnp.where(good, 1, 0)

    for x, y in own:
        pltpu.make_async_copy(loads_ref.at[:, x, y, :], stack.at[x, y, pl.ds(0, cols), :], local_sems.at[0]).start()
    mat_copy = pltpu.make_async_copy(mat_hbm, mat_ref, local_sems.at[1])
    mat_copy.start()
    moduli_copy = pltpu.make_async_copy(moduli_hbm, moduli_ref, local_sems.at[2])
    moduli_copy.start()

    vouches = max(sizes[2] - 2, 0) if direct else 0

    def vouch(round_):
        for dz in (-1, 1):
            @pl.when(exists((0, 0, dz)))
            def _():
                pl.semaphore_signal(vouch_sem.at[round_, 0 if dz > 0 else 1], inc=1, device_id=target((0, 0, dz)),
                                    device_id_type=pl.DeviceIdType.MESH)

    def vouched(round_):
        for dz in (-1, 1):
            @pl.when(exists((0, 0, dz)))
            def _():
                pl.semaphore_wait(vouch_sem.at[round_, 1 if dz > 0 else 0], 1)

    lane = lax.broadcasted_iota(jnp.int32, (1, LANES), 1)

    def spread(firsts, lasts, row, first, last, at):
        where_first, where_last = at + 2 * row, (at + 2 * row - 1) % LANES
        return (jnp.where(lane == where_first, pltpu.roll(first, where_first, 1), firsts),
                jnp.where(lane == where_last, pltpu.roll(last, (where_last + 1) % LANES, 1), lasts))

    mat_copy.wait()
    ids = jnp.concatenate([mat_ref[x] for x in range(nx)], axis=0)
    ids = (ids + 1).astype(F32)
    mats_rx[1, 1] = ids.astype(BF16)
    firsts = lasts = jnp.zeros((cols, LANES), F32)
    for x, y in own:
        row = x * ny + y
        first = jnp.broadcast_to(ids[row : row + 1, 0:LANES], (cols, LANES))
        last = jnp.broadcast_to(ids[row : row + 1, nz - LANES : nz], (cols, LANES))
        firsts, lasts = spread(firsts, lasts, row, first, last, IDS)
    whole = stack.at[:, :, pl.ds(0, cols), :]
    pltpu.make_async_copy(whole, whole, local_sems.at[0]).wait()
    for x, y in own:
        values = stack[x, y, 0:cols, :]
        padded[x + 1, y + 1] = values.astype(BF16)
        firsts, lasts = spread(firsts, lasts, x * ny + y, values[:, 0:LANES], values[:, nz - LANES : nz], 0)
    ends[0] = firsts.astype(BF16)
    ends[1] = lasts.astype(BF16)
    pl.semaphore_wait(barrier, expected)
    halo_start(0)
    if vouches:
        vouch(0)

    def gram(left, right):
        return tree_sum([dot(left(x, y), right(x, y), 1, 1) for x, y in own])

    def sum_copy(round_, number, peer):
        axes = plans[round_][number]
        count, index = group_of(axes)
        slot = offset_of(round_, number) + index
        return pltpu.make_async_remote_copy(
            src_ref=shares_of[round_].at[slot], dst_ref=shares_of[round_].at[slot],
            send_sem=sum_send.at[round_, number], recv_sem=sum_recv.at[round_, number],
            device_id=peer, device_id_type=pl.DeviceIdType.MESH,
        )

    def sum_start(round_, number, tile):
        axes = plans[round_][number]
        count, index = group_of(axes)
        shares_of[round_][offset_of(round_, number) + index] = tile
        if axes == AXES:
            plane = []
            for k in range(flat):
                there = lax.rem(spot + k, flat)
                plane.append((lax.div(there, sizes[1]), lax.rem(there, sizes[1])))
            low = 2 * me[2] < sizes[2]
            far, turn = jnp.where(low, sizes[2] - 1, 0), jnp.where(low, -1, 1)
            away = jnp.where(low, sizes[2] - 1 - me[2], me[2])
            for i in range(sizes[2] - 1):
                level = far + turn * (i + jnp.where(i < away, 0, 1))
                for gx, gy in plane[::-1]:
                    sum_copy(round_, number, {"gx": gx, "gy": gy, "gz": level}).start()
            for gx, gy in plane[:0:-1]:
                sum_copy(round_, number, {"gx": gx, "gy": gy, "gz": me[2]}).start()
        else:
            def send(k, carry):
                sum_copy(round_, number, peer_id(axes, lax.rem(index + k, count))).start()
                return carry

            each(count, send)

    def sum_wait(round_, number, sem):
        count, _ = group_of(plans[round_][number])
        if count > 1:
            part = shares_of[round_].at[pl.ds(0, count - 1)]
            pltpu.make_async_copy(part, part, sem.at[round_, number]).wait()

    def sum_finish(round_, number):
        sum_wait(round_, number, sum_recv)
        start = offset_of(round_, number)
        return tree_sum([shares_of[round_][start + peer] for peer in range(group_of(plans[round_][number])[0])])

    def sum_turn(round_):
        for number in range(1, len(plans[round_])):
            sum_start(round_, number, sum_finish(round_, number - 1))

    def sum_rest(round_):
        return sum_finish(round_, len(plans[round_]) - 1)

    def sum_left(round_):
        for number in range(len(plans[round_])):
            sum_wait(round_, number, sum_send)

    def loads_at(x, y):
        return stack[x, y, 0:cols, :]

    def image_at(x, y):
        return stack[x, y, cols:, :]

    square_part = gram(loads_at, loads_at)
    for round_ in range(1, vouches):
        vouched(round_ - 1)
        vouch(round_)
    if vouches:
        vouched(vouches - 1)
    moduli_copy.wait()

    def block_of(x, y):
        bx, lx = (0, nx - 1) if x == 0 else (2, 0) if x == nx + 1 else (1, x - 1)
        by, ly = (0, ny - 1) if y == 0 else (2, 0) if y == ny + 1 else (1, y - 1)
        return bx, by, lx * ny + ly

    odd = lax.rem(lane, 2) == 1

    def merged(edge):
        return {
            (bx, by): jnp.where(odd, edge[bx, by, 0].astype(F32), edge[bx, by, 1].astype(F32))
            for bx, by in itertools.product(range(3), repeat=2)
        }

    def tail_of(tiles, x, y, at=0):
        bx, by, row = block_of(x, y)
        return pltpu.roll(tiles[bx, by], (2 * LANES - at - 2 * row) % LANES, 1)

    def modulus_of(ids):
        return tree_sum([jnp.where(ids == float(number + 1), moduli_ref[number], 0.0) for number in range(mats)])

    halo_wait(0, halo_recv.at[0])
    full = nz + LANES
    tails = merged(ends_rx)
    flats = {key: modulus_of(mats_rx[key].astype(F32)) for key in tails}
    sides = {key: modulus_of(tile[0:8]) for key, tile in tails.items()}
    moduli = {}
    for x in xs:
        for y in ys:
            field[x, y] = jnp.concatenate([padded[x, y].astype(F32), tail_of(tails, x, y)], axis=1)
            bx, by, row = block_of(x, y)
            moduli[x, y] = jnp.concatenate([
                jnp.broadcast_to(flats[bx, by][row : row + 1, :], (8, nz)), tail_of(sides, x, y, IDS)
            ], axis=1)
    for x in range(nx + 1):
        for y in range(ny + 1):
            total = (moduli[x, y] + moduli[x, y + 1]) + (moduli[x + 1, y] + moduli[x + 1, y + 1])
            weight = 0.125 * (total + pltpu.roll(total, full - 1, 1))
            wt[x, y] = weight
            wtr[x, y] = pltpu.roll(weight, 1, 1)

    def double(tile):
        return jnp.concatenate([tile, tile], axis=0)

    def operate(direction_of, write):
        for x in range(nx):
            for y in range(ny):
                here = field[x + 1, y + 1]
                ahead = behind = flat = None
                w_ahead = w_behind = None
                for ex in (x, x + 1):
                    for ey in (y, y + 1):
                        corner_sum = (field[ex, ey] + field[ex, ey + 1]) + (field[ex + 1, ey] + field[ex + 1, ey + 1])
                        after, before = wt[ex, ey], wtr[ex, ey]
                        opposite = field[2 * ex - x, 2 * ey - y][:, 0:nz]
                        one = double(before) * corner_sum
                        two = double(after) * corner_sum
                        three = double((before + after)[:, 0:nz]) * opposite
                        ahead = one if ahead is None else ahead + one
                        behind = two if behind is None else behind + two
                        flat = three if flat is None else flat + three
                        w_ahead = before if w_ahead is None else w_ahead + before
                        w_behind = after if w_behind is None else w_behind + after
                ahead = ahead - double(w_ahead) * here
                behind = behind - double(w_behind) * here
                around = pltpu.roll(ahead, full - 1, 1)[:, 0:nz] + pltpu.roll(behind, 1, 1)[:, 0:nz] + flat
                centre = double((w_ahead + w_behind)[:, 0:nz]) * here[:, 0:nz]
                write(x, y, SIGMA * direction_of(x, y) + (k_far * around + k_self * centre))

    image_ends = [jnp.zeros((cols, LANES), F32)] * 2

    def write_first(x, y, image):
        stack[x, y, cols:, :] = image
        padded_im[x + 1, y + 1] = image.astype(BF16)
        image_ends[:] = spread(*image_ends, x * ny + y, image[:, 0:LANES], image[:, nz - LANES : nz], 0)

    operate(loads_at, write_first)
    ends_im[0] = image_ends[0].astype(BF16)
    ends_im[1] = image_ends[1].astype(BF16)
    halo_start(1)
    half = cols // 2
    both_part = gram(image_at, lambda x, y: stack[x, y])
    near_part = gram(image_at, lambda x, y: padded[x + 1, y + 1].astype(F32))
    parts = jnp.concatenate(
        [square_part, both_part, near_part, jnp.zeros((cols, LANES - 4 * cols), F32)], axis=1
    )
    sum_start(0, 0, jnp.where(lane < LANES // 2, parts[0:half], pltpu.roll(parts[half:], LANES // 2, 1)))
    sum_turn(0)

    halo_wait(1, halo_recv.at[1])
    tails_im = merged(ends_im_rx)
    for x in xs:
        for y in ys:
            inner = 1 <= x <= nx and 1 <= y <= ny
            value = image_at(x - 1, y - 1) if inner else padded_im[x, y].astype(F32)
            field[x, y] = jnp.concatenate([value, tail_of(tails_im, x, y)], axis=1)
    last_parts = []

    def write_last(x, y, image):
        last_parts.append(dot(image_at(x, y), image, 1, 1))

    operate(image_at, write_last)
    sum_start(1, 0, pack(tree_sum(last_parts)))

    tile = sum_rest(0)
    table = jnp.concatenate([tile, pltpu.roll(tile, LANES // 2, 1)], axis=0)
    square, cross, quad, near = (table[:, cols * k : cols * (k + 1)] for k in range(4))
    cross = 0.5 * (cross + cross.T)
    near = 0.5 * (near + near.T)
    row_id = lax.broadcasted_iota(jnp.int32, (cols, cols), 0)
    col_id = lax.broadcasted_iota(jnp.int32, (cols, cols), 1)
    eye = jnp.where(row_id == col_id, 1.0, 0.0)
    inverse = solve(square, eye)
    alpha = solve(cross, square)
    updated = square + dot(alpha, dot(quad, alpha, 1, 0) - cross, 0, 0) - dot(cross, alpha, 0, 0)
    grown = eye + dot(inverse, updated, 1, 0)
    alpha_t = alpha.T
    mix = jnp.concatenate([grown.T, -alpha_t], axis=1)
    mix_hi = mix.astype(BF16)
    mix_lo = (mix - mix_hi.astype(F32)).astype(BF16)
    mix_both = jnp.concatenate([mix_hi, mix_lo], axis=0)
    known = dot(grown, dot(near, grown, 1, 0) - dot(quad, alpha, 1, 0), 0, 0) - dot(alpha, dot(quad, grown, 1, 0), 0, 0)

    for x in xs:
        for y in ys:
            inner = 1 <= x <= nx and 1 <= y <= ny
            near_tail = jnp.concatenate([
                tail_of(tails, x, y).astype(BF16), tail_of(tails_im, x, y).astype(BF16)
            ], axis=0)
            if not inner:
                near_tail = jnp.concatenate([
                    jnp.concatenate([padded[x, y], padded_im[x, y]], axis=0), near_tail
                ], axis=1)
            twice = dot(mix_both, near_tail, 1, 0, None)
            mixed = twice[0:cols] + twice[cols:]
            if inner:
                direction = dot(mix, stack[x - 1, y - 1], 1, 0)
                pair_ref[x - 1, y - 1, 0:cols, :] = direction
                mixed = jnp.concatenate([direction, mixed], axis=1)
            field[x, y] = mixed.astype(BF16).astype(F32)

    def write_second(x, y, image):
        pair_ref[x, y, cols:, :] = image

    operate(lambda x, y: pair_ref[x, y, 0:cols, :], write_second)
    for x, y in own:
        base_ref[x, y, 0:cols, :] = dot(alpha_t, stack[x, y, 0:cols, :], 1, 0)
        base_ref[x, y, cols:, :] = stack[x, y, 0:cols, :] - dot(alpha_t, stack[x, y, cols:, :], 1, 0)
    halo_wait(0, halo_send.at[0])
    halo_wait(1, halo_send.at[1])
    sum_left(0)
    sum_turn(1)
    last = unpack(sum_rest(1), cols)
    total = known + dot(alpha, dot(last, alpha, 1, 0), 0, 0)
    coef_ref[...] = solve(0.5 * (total + total.T), updated).T
    sum_left(1)


def last_body(coef_ref, base_ref, pair_ref, sol_ref, res_ref, stage, sems):
    cols, nx, ny, nz = sol_ref.shape
    coef = coef_ref[...]
    for x, y in itertools.product(range(nx), range(ny)):
        for which, ref, sign in ((0, sol_ref, 1.0), (1, res_ref, -1.0)):
            rows = slice(which * cols, (which + 1) * cols)
            stage[which, x, y] = base_ref[x, y, rows, :] + sign * dot(coef, pair_ref[x, y, rows, :], 1, 0)
            pltpu.make_async_copy(stage.at[which, x, y], ref.at[:, x, y, :], sems.at[which]).start()
    for which in range(2):
        pltpu.make_async_copy(stage.at[which], stage.at[which], sems.at[which]).wait()


def on_device(sizes, loads, moduli, material):
    cols, nx, ny, nz = loads.shape
    count = int(np.prod(sizes))
    split = (("gx", "gy"), ("gz",))
    plans = (split, (AXES,) if count <= DIRECT_LIMIT else split)

    def slots(phases):
        return sum(int(np.prod([sizes[AXES.index(a)] for a in axes])) for axes in phases)

    vmem = pl.BlockSpec(memory_space=pltpu.VMEM)
    anywhere = pl.BlockSpec(memory_space=pl.ANY)
    full = nz + LANES
    credits = (nz // LANES) * 2 * (nx + ny + 2) + 18 + 8 * (nx * ny * nz // (cols * LANES))
    base, pair, coef = pl.pallas_call(
        functools.partial(main_body, sizes, plans, stiffness_values()),
        out_shape=(
            pltpu.VMEM((nx, ny, 2 * cols, nz), F32),
            pltpu.VMEM((nx, ny, 2 * cols, nz), F32),
            pltpu.VMEM((cols, cols), F32),
        ),
        in_specs=[anywhere, anywhere, anywhere],
        out_specs=(vmem, vmem, vmem),
        scratch_shapes=[
            pltpu.VMEM((nx, ny, 2 * cols, nz), F32),
            pltpu.VMEM((nx + 2, ny + 2, cols, nz), BF16),
            pltpu.VMEM((nx + 2, ny + 2, cols, nz), BF16),
            pltpu.VMEM((3, 3, nx * ny, nz), BF16),
            pltpu.VMEM((2, cols, LANES), BF16),
            pltpu.VMEM((3, 3, 2, cols, LANES), BF16),
            pltpu.VMEM((2, cols, LANES), BF16),
            pltpu.VMEM((3, 3, 2, cols, LANES), BF16),
            pltpu.VMEM((nx + 2, ny + 2, cols, full), F32),
            pltpu.VMEM((nx + 1, ny + 1, 8, full), F32),
            pltpu.VMEM((nx + 1, ny + 1, 8, full), F32),
            pltpu.VMEM((slots(plans[0]), cols // 2, LANES), F32),
            pltpu.VMEM((slots(plans[1]), cols * cols // LANES, LANES), F32),
            pltpu.SMEM(moduli.shape, F32),
            pltpu.VMEM(material.shape, jnp.int32),
            pltpu.VMEM((credits, cols, LANES), BF16),
            pltpu.SemaphoreType.DMA((2,)),
            pltpu.SemaphoreType.DMA((2,)),
            pltpu.SemaphoreType.DMA((2, 2)),
            pltpu.SemaphoreType.DMA((2, 2)),
            pltpu.SemaphoreType.DMA((3,)),
            pltpu.SemaphoreType.REGULAR((max(sizes[2] - 2, 1) if count <= DIRECT_LIMIT else 1, 2)),
        ],
        compiler_params=pltpu.CompilerParams(collective_id=0, has_side_effects=True),
    )(moduli, loads, material)
    out = jax.ShapeDtypeStruct(loads.shape, F32)
    return pl.pallas_call(
        last_body,
        out_shape=(out, out),
        in_specs=[vmem, vmem, vmem],
        out_specs=(anywhere, anywhere),
        scratch_shapes=[pltpu.VMEM((2, nx, ny, cols, nz), F32), pltpu.SemaphoreType.DMA((2,))],
        compiler_params=pltpu.CompilerParams(vmem_limit_bytes=4 * 2**20),
    )(coef, base, pair)


def solution(mesh):
    sizes = tuple(mesh.shape[axis] for axis in AXES)
    in_specs = (P(None, "gx", "gy", "gz"), P(), P("gx", "gy", "gz"))
    out_specs = (P(None, "gx", "gy", "gz"), P(None, "gx", "gy", "gz"))
    return jax.shard_map(
        functools.partial(on_device, sizes), mesh=mesh, in_specs=in_specs, out_specs=out_specs, check_vma=False
    )
```

time: 35.3 us -> 24.8 us (0.70)
  Pallas kernels: 33.1 us -> 23.9 us
  local copies, waits for them, and re-layouts: 1.31 us -> 0 us
    pallas_call x1 -> x2, Pallas kernels: 33.1 us -> 23.9 us  [the longest x1 20.7 us: on_device(): pl.pallas_call(functools.partial(main_body, sizes, plans, stiffness_value...]
    unnamed x2 -> x0, local copies, waits for them, and re-layouts: 1.31 us -> none
where the time goes in v1:
time: 24.8 us; the launch traced here: 24.6 us
  Pallas kernels  23.9 us (96%)
  between operations  0.64 us (3%)
    pallas_call x1, Pallas kernels, on_device(): pl.pallas_call(functools.partial(main_body, sizes, plans, stiffness_value...  20.7 us
    pallas_call x1, Pallas kernels, on_device(): pl.pallas_call(last_body, out_shape=(out, out), in_specs=[vmem, vmem, vme...  3.25 us

profile of v1, /device:TPU:0, one launch (start us, length us, event | category | flops | bytes accessed | tf_op | source)
XLA Modules:
  0.0 24.6 jit_solution(13774433003597544036)
XLA Ops:
  0.6 20.7 %shard_map.50 = (f32[2,4,32,256]{3,2,1,0:T(8,128)S(1)}, f32[2,4,32,256]{3,2,1,0:T(8,128)S(1)}, f32[16,16]{1,0:T(8,128)S(1)}) custom-call(f32[8]{0:T(128)} %moduli_hbm.1, f32[16,2,4,256]{3,2,1,0:T(4,128)} %loads_ref.1, s32[2,4,256]{2,1,0:T(4,128)} %mat_hbm.1), custom_call_target="tpu_custom_call" | custom-call | tf_op jit(solution)/shard_map/pallas_call | solution.py:564
  21.3 3.3 %shard_map.51 = (f32[16,2,4,256]{3,2,1,0:T(4,128)}, f32[16,2,4,256]{3,2,1,0:T(4,128)}) custom-call(f32[16,16]{1,0:T(8,128)S(1)} %get-tuple-element.5.coef_ref, f32[2,4,32,256]{3,2,1,0:T(8,128)S(1)} %get-tuple-element.6.base_ref, f32[2,4,32,256]{3,2,1,0:T(8,128)S(1)} %get-tuple-element.7.pair_ref), custom_call_target="tpu_custom_call" | custom-call | tf_op jit(solution)/shard_map/pallas_call | solution.py:600

commit v2 on v1

--- a/solution.py
+++ b/solution.py
@@ -90,16 +90,16 @@
 
 def main_body(sizes, plans, stiff, moduli_hbm, loads_ref, mat_hbm, base_ref, pair_ref, coef_ref,
               stack, padded, padded_im, mats_rx, ends, ends_rx, ends_im, ends_im_rx, field, wt, wtr,
-              shares_table, shares_last, moduli_ref, mat_ref, credit,
+              shares_square, shares_table, shares_last, tail_im, moduli_ref, mat_ref, credit,
               halo_send, halo_recv, sum_send, sum_recv, local_sems, vouch_sem):
     cols, nx, ny, nz = loads_ref.shape
     mats = moduli_ref.shape[0]
     me = [lax.axis_index(axis) for axis in AXES]
     k_self, k_edge, k_far = stiff[0], stiff[1], stiff[2]
     assert k_edge == 0.0 and stiff[2] == stiff[3]
-    assert 2 * nx * ny <= IDS and (nx * ny * nz) % (cols * LANES) == 0 and nz % LANES == 0
+    assert 4 * nx * ny <= IDS and (nx * ny * nz) % (cols * LANES) == 0 and nz % LANES == 0
     xs, ys = range(nx + 2), range(ny + 2)
-    shares_of = (shares_table, shares_last)
+    shares_of = (shares_square, shares_table, shares_last)
     own = list(itertools.product(range(nx), range(ny)))
 
     directions = [
@@ -123,7 +123,7 @@
         return 1 - direction[0], 1 - direction[1]
 
     def halo_start(round_):
-        core, source, edge = ((padded, ends, ends_rx), (padded_im, ends_im, ends_im_rx))[round_]
+        core = (padded, padded_im)[round_]
         for direction in directions:
             dx, dy, dz = direction
             pairs = []
@@ -135,8 +135,12 @@
                 pairs.append((core.at[src_x, src_y], core.at[dst_x, dst_y]))
                 if round_ == 0:
                     pairs.append((mats_rx.at[1, 1], mats_rx.at[place(direction)]))
+                else:
+                    pairs.insert(0, (ends_im, ends_im_rx.at[place(direction)]))
+            elif round_ == 0:
+                pairs.append((ends.at[1 if dz > 0 else 0], ends_rx.at[(*place(direction), 0 if dz > 0 else 1)]))
             else:
-                pairs.append((source.at[1 if dz > 0 else 0], edge.at[(*place(direction), 0 if dz > 0 else 1)]))
+                continue
 
             @pl.when(exists(direction))
             def _():
@@ -153,9 +157,11 @@
         choices = [(0,) if size == 1 else (1,) if size == 2 else (1, 2) for size in sizes]
         per = nz // LANES
         for cx, cy, cz in itertools.product(*choices):
-            total = per * (cx * ny + cy * nx + cx * cy) + cz * (1 + cx) * (1 + cy)
+            total = per * (cx * ny + cy * nx + cx * cy)
             if round_ == 0:
-                total += (cx + cy + cx * cy) * (nx * ny * nz // (cols * LANES))
+                total += (cx + cy + cx * cy) * (nx * ny * nz // (cols * LANES)) + cz * (1 + cx) * (1 + cy)
+            else:
+                total += cx + cy + cx * cy
             if total:
                 tests = [numbers[i] == c for i, c in enumerate((cx, cy, cz)) if len(choices[i]) > 1]
 
@@ -199,8 +205,8 @@
     for bx, by in itertools.product(range(3), repeat=2):
         for side in range(2):
             ends_rx[bx, by, side] = jnp.zeros(ends_rx.shape[3:], BF16)
-            ends_im_rx[bx, by, side] = jnp.zeros(ends_im_rx.shape[3:], BF16)
         if (bx, by) != (1, 1):
+            ends_im_rx[bx, by] = jnp.zeros(ends_im_rx.shape[2:], BF16)
             mats_rx[bx, by] = jnp.zeros(mats_rx.shape[2:], BF16)
     for x in xs:
         for y in ys:
@@ -278,9 +284,12 @@
     lane = lax.broadcasted_iota(jnp.int32, (1, LANES), 1)
 
     def spread(firsts, lasts, row, first, last, at):
-        where_first, where_last = at + 2 * row, (at + 2 * row - 1) % LANES
-        return (jnp.where(lane == where_first, pltpu.roll(first, where_first, 1), firsts),
-                jnp.where(lane == where_last, pltpu.roll(last, (where_last + 1) % LANES, 1), lasts))
+        spot = at + 4 * row
+        ahead = jnp.logical_and(lane >= spot, lane < spot + 2)
+        start = (spot - 2) % LANES
+        behind = jnp.logical_and(lane >= start, lane < start + 2)
+        return (jnp.where(ahead, pltpu.roll(first, spot, 1), firsts),
+                jnp.where(behind, pltpu.roll(last, spot, 1), lasts))
 
     mat_copy.wait()
     ids = jnp.concatenate([mat_ref[x] for x in range(nx)], axis=0)
@@ -372,11 +381,10 @@
         return stack[x, y, cols:, :]
 
     square_part = gram(loads_at, loads_at)
+    sum_start(0, 0, pack(square_part))
     for round_ in range(1, vouches):
         vouched(round_ - 1)
         vouch(round_)
-    if vouches:
-        vouched(vouches - 1)
     moduli_copy.wait()
 
     def block_of(x, y):
@@ -384,7 +392,7 @@
         by, ly = (0, ny - 1) if y == 0 else (2, 0) if y == ny + 1 else (1, y - 1)
         return bx, by, lx * ny + ly
 
-    odd = lax.rem(lane, 2) == 1
+    odd = lax.rem(lane, 4) >= 2
 
     def merged(edge):
         return {
@@ -394,7 +402,7 @@
 
     def tail_of(tiles, x, y, at=0):
         bx, by, row = block_of(x, y)
-        return pltpu.roll(tiles[bx, by], (2 * LANES - at - 2 * row) % LANES, 1)
+        return pltpu.roll(tiles[bx, by], (2 * LANES - at - 4 * row) % LANES, 1)
 
     def modulus_of(ids):
         return tree_sum([jnp.where(ids == float(number + 1), moduli_ref[number], 0.0) for number in range(mats)])
@@ -422,7 +430,8 @@
     def double(tile):
         return jnp.concatenate([tile, tile], axis=0)
 
-    def operate(direction_of, write):
+    def operate(direction_of, write, width=None):
+        width = width or nz
         for x in range(nx):
             for y in range(ny):
                 here = field[x + 1, y + 1]
@@ -432,10 +441,10 @@
                     for ey in (y, y + 1):
                         corner_sum = (field[ex, ey] + field[ex, ey + 1]) + (field[ex + 1, ey] + field[ex + 1, ey + 1])
                         after, before = wt[ex, ey], wtr[ex, ey]
-                        opposite = field[2 * ex - x, 2 * ey - y][:, 0:nz]
+                        opposite = field[2 * ex - x, 2 * ey - y][:, 0:width]
                         one = double(before) * corner_sum
                         two = double(after) * corner_sum
-                        three = double((before + after)[:, 0:nz]) * opposite
+                        three = double((before + after)[:, 0:width]) * opposite
                         ahead = one if ahead is None else ahead + one
                         behind = two if behind is None else behind + two
                         flat = three if flat is None else flat + three
@@ -443,54 +452,65 @@
                         w_behind = after if w_behind is None else w_behind + after
                 ahead = ahead - double(w_ahead) * here
                 behind = behind - double(w_behind) * here
-                around = pltpu.roll(ahead, full - 1, 1)[:, 0:nz] + pltpu.roll(behind, 1, 1)[:, 0:nz] + flat
-                centre = double((w_ahead + w_behind)[:, 0:nz]) * here[:, 0:nz]
+                around = pltpu.roll(ahead, full - 1, 1)[:, 0:width] + pltpu.roll(behind, 1, 1)[:, 0:width] + flat
+                centre = double((w_ahead + w_behind)[:, 0:width]) * here[:, 0:width]
                 write(x, y, SIGMA * direction_of(x, y) + (k_far * around + k_self * centre))
 
-    image_ends = [jnp.zeros((cols, LANES), F32)] * 2
+    has_right = (me[2] < sizes[2] - 1).astype(jnp.int32)
+    has_left = (me[2] > 0).astype(jnp.int32)
+    beyond = jnp.logical_or(lane < has_right, lane >= LANES - has_left)
+    image_ends = [jnp.zeros((cols, LANES), F32)]
 
     def write_first(x, y, image):
-        stack[x, y, cols:, :] = image
-        padded_im[x + 1, y + 1] = image.astype(BF16)
-        image_ends[:] = spread(*image_ends, x * ny + y, image[:, 0:LANES], image[:, nz - LANES : nz], 0)
-
-    operate(loads_at, write_first)
-    ends_im[0] = image_ends[0].astype(BF16)
-    ends_im[1] = image_ends[1].astype(BF16)
+        row = x * ny + y
+        stack[x, y, cols:, :] = image[:, 0:nz]
+        padded_im[x + 1, y + 1] = image[:, 0:nz].astype(BF16)
+        tail = jnp.where(beyond, image[:, nz:], 0.0)
+        tail_im[x, y] = tail
+        turned = pltpu.roll(tail, 4 * row, 1)
+        image_ends[0] = image_ends[0] + turned
+
+    operate(lambda x, y: jnp.concatenate([loads_at(x, y), field[x + 1, y + 1][:, nz:]], axis=1), write_first, full)
+    ends_im[...] = image_ends[0].astype(BF16)
     halo_start(1)
-    half = cols // 2
     both_part = gram(image_at, lambda x, y: stack[x, y])
-    near_part = gram(image_at, lambda x, y: padded[x + 1, y + 1].astype(F32))
-    parts = jnp.concatenate(
-        [square_part, both_part, near_part, jnp.zeros((cols, LANES - 4 * cols), F32)], axis=1
-    )
-    sum_start(0, 0, jnp.where(lane < LANES // 2, parts[0:half], pltpu.roll(parts[half:], LANES // 2, 1)))
+    if vouches:
+        vouched(vouches - 1)
+    sum_start(1, 0, jnp.concatenate([pack(both_part[:, 0:cols]), pack(both_part[:, cols:])], axis=0))
     sum_turn(0)
 
     halo_wait(1, halo_recv.at[1])
-    tails_im = merged(ends_im_rx)
+    turned_im = {}
+    for x in xs:
+        for y in ys:
+            if 1 <= x <= nx and 1 <= y <= ny:
+                turned_im[x, y] = tail_im[x - 1, y - 1]
+            else:
+                bx, by, row = block_of(x, y)
+                turned_im[x, y] = pltpu.roll(ends_im_rx[bx, by].astype(F32), (LANES - 4 * row) % LANES, 1)
     for x in xs:
         for y in ys:
             inner = 1 <= x <= nx and 1 <= y <= ny
             value = image_at(x - 1, y - 1) if inner else padded_im[x, y].astype(F32)
-            field[x, y] = jnp.concatenate([value, tail_of(tails_im, x, y)], axis=1)
+            field[x, y] = jnp.concatenate([value, turned_im[x, y]], axis=1)
     last_parts = []
 
     def write_last(x, y, image):
         last_parts.append(dot(image_at(x, y), image, 1, 1))
 
     operate(image_at, write_last)
-    sum_start(1, 0, pack(tree_sum(last_parts)))
-
-    tile = sum_rest(0)
-    table = jnp.concatenate([tile, pltpu.roll(tile, LANES // 2, 1)], axis=0)
-    square, cross, quad, near = (table[:, cols * k : cols * (k + 1)] for k in range(4))
-    cross = 0.5 * (cross + cross.T)
-    near = 0.5 * (near + near.T)
+    sum_start(2, 0, pack(tree_sum(last_parts)))
+
+    square = unpack(sum_rest(0), cols)
+    sum_turn(1)
     row_id = lax.broadcasted_iota(jnp.int32, (cols, cols), 0)
     col_id = lax.broadcasted_iota(jnp.int32, (cols, cols), 1)
     eye = jnp.where(row_id == col_id, 1.0, 0.0)
     inverse = solve(square, eye)
+    table = sum_rest(1)
+    half = table.shape[0] // 2
+    cross, quad = unpack(table[0:half], cols), unpack(table[half:], cols)
+    cross = 0.5 * (cross + cross.T)
     alpha = solve(cross, square)
     updated = square + dot(alpha, dot(quad, alpha, 1, 0) - cross, 0, 0) - dot(cross, alpha, 0, 0)
     grown = eye + dot(inverse, updated, 1, 0)
@@ -499,13 +519,15 @@
     mix_hi = mix.astype(BF16)
     mix_lo = (mix - mix_hi.astype(F32)).astype(BF16)
     mix_both = jnp.concatenate([mix_hi, mix_lo], axis=0)
-    known = dot(grown, dot(near, grown, 1, 0) - dot(quad, alpha, 1, 0), 0, 0) - dot(alpha, dot(quad, grown, 1, 0), 0, 0)
+    known = dot(grown, dot(cross, grown, 1, 0) - dot(quad, alpha, 1, 0), 0, 0) - dot(alpha, dot(quad, grown, 1, 0), 0, 0)
+
+    known = 0.5 * (known + known.T)
 
     for x in xs:
         for y in ys:
             inner = 1 <= x <= nx and 1 <= y <= ny
             near_tail = jnp.concatenate([
-                tail_of(tails, x, y).astype(BF16), tail_of(tails_im, x, y).astype(BF16)
+                tail_of(tails, x, y).astype(BF16), turned_im[x, y].astype(BF16)
             ], axis=0)
             if not inner:
                 near_tail = jnp.concatenate([
@@ -529,21 +551,25 @@
     halo_wait(0, halo_send.at[0])
     halo_wait(1, halo_send.at[1])
     sum_left(0)
-    sum_turn(1)
-    last = unpack(sum_rest(1), cols)
-    total = known + dot(alpha, dot(last, alpha, 1, 0), 0, 0)
-    coef_ref[...] = solve(0.5 * (total + total.T), updated).T
     sum_left(1)
+    sum_turn(2)
+    last = unpack(sum_rest(2), cols)
+    turned = dot(alpha_t, last, 1, 0) + dot(alpha_t, last, 1, 1)
+    coef_ref[...] = solve(known + 0.5 * dot(turned, alpha, 1, 0), updated).T
+    sum_left(2)
 
 
 def last_body(coef_ref, base_ref, pair_ref, sol_ref, res_ref, stage, sems):
     cols, nx, ny, nz = sol_ref.shape
     coef = coef_ref[...]
-    for x, y in itertools.product(range(nx), range(ny)):
+    for x in range(nx):
         for which, ref, sign in ((0, sol_ref, 1.0), (1, res_ref, -1.0)):
             rows = slice(which * cols, (which + 1) * cols)
-            stage[which, x, y] = base_ref[x, y, rows, :] + sign * dot(coef, pair_ref[x, y, rows, :], 1, 0)
-            pltpu.make_async_copy(stage.at[which, x, y], ref.at[:, x, y, :], sems.at[which]).start()
+            for y in range(ny):
+                stage[which, :, x, y, :] = (
+                    base_ref[x, y, rows, :] + sign * dot(coef, pair_ref[x, y, rows, :], 1, 0)
+                )
+            pltpu.make_async_copy(stage.at[which, :, x], ref.at[:, x], sems.at[which]).start()
     for which in range(2):
         pltpu.make_async_copy(stage.at[which], stage.at[which], sems.at[which]).wait()
 
@@ -552,7 +578,8 @@
     cols, nx, ny, nz = loads.shape
     count = int(np.prod(sizes))
     split = (("gx", "gy"), ("gz",))
-    plans = (split, (AXES,) if count <= DIRECT_LIMIT else split)
+    quick = (AXES,) if count <= DIRECT_LIMIT else split
+    plans = (split, quick, quick)
 
     def slots(phases):
         return sum(int(np.prod([sizes[AXES.index(a)] for a in axes])) for axes in phases)
@@ -577,20 +604,22 @@
             pltpu.VMEM((3, 3, nx * ny, nz), BF16),
             pltpu.VMEM((2, cols, LANES), BF16),
             pltpu.VMEM((3, 3, 2, cols, LANES), BF16),
-            pltpu.VMEM((2, cols, LANES), BF16),
-            pltpu.VMEM((3, 3, 2, cols, LANES), BF16),
+            pltpu.VMEM((cols, LANES), BF16),
+            pltpu.VMEM((3, 3, cols, LANES), BF16),
             pltpu.VMEM((nx + 2, ny + 2, cols, full), F32),
             pltpu.VMEM((nx + 1, ny + 1, 8, full), F32),
             pltpu.VMEM((nx + 1, ny + 1, 8, full), F32),
-            pltpu.VMEM((slots(plans[0]), cols // 2, LANES), F32),
-            pltpu.VMEM((slots(plans[1]), cols * cols // LANES, LANES), F32),
+            pltpu.VMEM((slots(plans[0]), cols * cols // LANES, LANES), F32),
+            pltpu.VMEM((slots(plans[1]), 2 * cols * cols // LANES, LANES), F32),
+            pltpu.VMEM((slots(plans[2]), cols * cols // LANES, LANES), F32),
+            pltpu.VMEM((nx, ny, cols, LANES), F32),
             pltpu.SMEM(moduli.shape, F32),
             pltpu.VMEM(material.shape, jnp.int32),
             pltpu.VMEM((credits, cols, LANES), BF16),
             pltpu.SemaphoreType.DMA((2,)),
             pltpu.SemaphoreType.DMA((2,)),
-            pltpu.SemaphoreType.DMA((2, 2)),
-            pltpu.SemaphoreType.DMA((2, 2)),
+            pltpu.SemaphoreType.DMA((3, 2)),
+            pltpu.SemaphoreType.DMA((3, 2)),
             pltpu.SemaphoreType.DMA((3,)),
             pltpu.SemaphoreType.REGULAR((max(sizes[2] - 2, 1) if count <= DIRECT_LIMIT else 1, 2)),
         ],
@@ -602,7 +631,7 @@
         out_shape=(out, out),
         in_specs=[vmem, vmem, vmem],
         out_specs=(anywhere, anywhere),
-        scratch_shapes=[pltpu.VMEM((2, nx, ny, cols, nz), F32), pltpu.SemaphoreType.DMA((2,))],
+        scratch_shapes=[pltpu.VMEM((2, cols, nx, ny, nz), F32), pltpu.SemaphoreType.DMA((2,))],
         compiler_params=pltpu.CompilerParams(vmem_limit_bytes=4 * 2**20),
     )(coef, base, pair)
 

time: 24.8 us -> 20.7 us (0.83)
  Pallas kernels: 23.9 us -> 19.9 us
    pallas_call x1, Pallas kernels: 3.25 us -> 1.09 us  [on_device(): pl.pallas_call(last_body, out_shape=(out, out), in_specs=[vmem, vmem, vme...]
    pallas_call x1, Pallas kernels: 20.7 us -> 18.8 us  [on_device(): pl.pallas_call(functools.partial(main_body, sizes, plans, stiffness_value...]
where the time goes in v2:
time: 20.7 us; the launch traced here: 20.5 us
  Pallas kernels  19.9 us (96%)
  between operations  0.64 us (3%)
    pallas_call x1, Pallas kernels, on_device(): pl.pallas_call(functools.partial(main_body, sizes, plans, stiffness_value...  18.8 us
    pallas_call x1, Pallas kernels, on_device(): pl.pallas_call(last_body, out_shape=(out, out), in_specs=[vmem, vmem, vme...  1.09 us

profile of v2, /device:TPU:0, one launch (start us, length us, event | category | flops | bytes accessed | tf_op | source)
XLA Modules:
  0.0 20.5 jit_solution(11717836211943697931)
XLA Ops:
  0.6 18.8 %shard_map.50 = (f32[2,4,32,256]{3,2,1,0:T(8,128)S(1)}, f32[2,4,32,256]{3,2,1,0:T(8,128)S(1)}, f32[16,16]{1,0:T(8,128)S(1)}) custom-call(f32[8]{0:T(128)} %moduli_hbm.1, f32[16,2,4,256]{3,2,1,0:T(4,128)} %loads_ref.1, s32[2,4,256]{2,1,0:T(4,128)} %mat_hbm.1), custom_call_target="tpu_custom_call" | custom-call | tf_op jit(solution)/shard_map/pallas_call | solution.py:591
  19.4 1.1 %shard_map.51 = (f32[16,2,4,256]{3,2,1,0:T(4,128)}, f32[16,2,4,256]{3,2,1,0:T(4,128)}) custom-call(f32[16,16]{1,0:T(8,128)S(1)} %get-tuple-element.5.coef_ref, f32[2,4,32,256]{3,2,1,0:T(8,128)S(1)} %get-tuple-element.6.base_ref, f32[2,4,32,256]{3,2,1,0:T(8,128)S(1)} %get-tuple-element.7.pair_ref), custom_call_target="tpu_custom_call" | custom-call | tf_op jit(solution)/shard_map/pallas_call | solution.py:629

commit v3 on v2

--- a/solution.py
+++ b/solution.py
@@ -17,6 +17,7 @@
 LANES = 128
 DIRECT_LIMIT = 32
 IDS = 64
+TILE_UNITS = 64
 
 
 def stiffness_values():
@@ -82,6 +83,17 @@
     return jnp.concatenate(right, axis=0)[:, 0 : rhs.shape[1]]
 
 
+def halves(value):
+    high = value.astype(BF16)
+    return high, (value - high.astype(F32)).astype(BF16)
+
+
+def split_dot(left_high, left_low, right_high, right_low, left_dim, right_dim):
+    rows = left_high.shape[0]
+    both = dot(jnp.concatenate([left_high, left_low], axis=0), right_high, left_dim, right_dim, None)
+    return both[0:rows] + both[rows:] + dot(left_high, right_low, left_dim, right_dim, None)
+
+
 def tree_sum(terms):
     while len(terms) > 1:
         terms = [a + b for a, b in zip(terms[0::2], terms[1::2])] + terms[len(terms) & ~1 :]
@@ -89,15 +101,15 @@
 
 
 def main_body(sizes, plans, stiff, moduli_hbm, loads_ref, mat_hbm, base_ref, pair_ref, coef_ref,
-              stack, padded, padded_im, mats_rx, ends, ends_rx, ends_im, ends_im_rx, field, wt, wtr,
+              stack, low, padded, padded_im, mats_rx, ends, ends_rx, ends_im, ends_im_rx, field, wt, wtr, level, node,
               shares_square, shares_table, shares_last, tail_im, moduli_ref, mat_ref, credit,
-              halo_send, halo_recv, sum_send, sum_recv, local_sems, vouch_sem):
+              sent, halo_recv, sum_recv, local_sems, vouch_sem):
     cols, nx, ny, nz = loads_ref.shape
     mats = moduli_ref.shape[0]
     me = [lax.axis_index(axis) for axis in AXES]
     k_self, k_edge, k_far = stiff[0], stiff[1], stiff[2]
     assert k_edge == 0.0 and stiff[2] == stiff[3]
-    assert 4 * nx * ny <= IDS and (nx * ny * nz) % (cols * LANES) == 0 and nz % LANES == 0
+    assert 4 * nx * ny <= IDS and (nx * ny * nz) % (cols * LANES) == 0 and nz % LANES == 0 and TILE_UNITS % cols == 0
     xs, ys = range(nx + 2), range(ny + 2)
     shares_of = (shares_square, shares_table, shares_last)
     own = list(itertools.product(range(nx), range(ny)))
@@ -146,29 +158,32 @@
             def _():
                 for src, dst in pairs:
                     pltpu.make_async_remote_copy(
-                        src_ref=src, dst_ref=dst, send_sem=halo_send.at[round_], recv_sem=halo_recv.at[round_],
+                        src_ref=src, dst_ref=dst, send_sem=sent, recv_sem=halo_recv.at[round_],
                         device_id=target(direction), device_id_type=pl.DeviceIdType.MESH,
                     ).start()
 
-    def halo_wait(round_, sem):
+    def wait_units(total, sem):
+        part = credit.at[pl.ds(0, total)]
+        pltpu.make_async_copy(part, part, sem).wait()
+
+    def halo_wait(rounds, sem, more=0):
         numbers = [
             ((me[i] > 0).astype(jnp.int32) + (me[i] < sizes[i] - 1).astype(jnp.int32)) for i in range(3)
         ]
         choices = [(0,) if size == 1 else (1,) if size == 2 else (1, 2) for size in sizes]
         per = nz // LANES
         for cx, cy, cz in itertools.product(*choices):
-            total = per * (cx * ny + cy * nx + cx * cy)
-            if round_ == 0:
-                total += (cx + cy + cx * cy) * (nx * ny * nz // (cols * LANES)) + cz * (1 + cx) * (1 + cy)
-            else:
-                total += cx + cy + cx * cy
+            total = 0
+            for round_ in rounds:
+                total += per * (cx * ny + cy * nx + cx * cy)
+                if round_ == 0:
+                    total += (cx + cy + cx * cy) * (nx * ny * nz // (cols * LANES)) + cz * (1 + cx) * (1 + cy)
+                else:
+                    total += cx + cy + cx * cy
+            total = total * TILE_UNITS // cols + more
             if total:
                 tests = [numbers[i] == c for i, c in enumerate((cx, cy, cz)) if len(choices[i]) > 1]
-
-                def take():
-                    part = credit.at[pl.ds(0, total)]
-                    pltpu.make_async_copy(part, part, sem).wait()
-
+                take = functools.partial(wait_units, total, sem)
                 if tests:
                     pl.when(functools.reduce(jnp.logical_and, tests))(take)
                 else:
@@ -201,18 +216,6 @@
         return sum(group_of(axes)[0] for axes in plans[round_][:number])
 
     direct = (AXES,) in plans
-
-    for bx, by in itertools.product(range(3), repeat=2):
-        for side in range(2):
-            ends_rx[bx, by, side] = jnp.zeros(ends_rx.shape[3:], BF16)
-        if (bx, by) != (1, 1):
-            ends_im_rx[bx, by] = jnp.zeros(ends_im_rx.shape[2:], BF16)
-            mats_rx[bx, by] = jnp.zeros(mats_rx.shape[2:], BF16)
-    for x in xs:
-        for y in ys:
-            if not (1 <= x <= nx and 1 <= y <= ny):
-                padded[x, y] = jnp.zeros(padded.shape[2:], BF16)
-                padded_im[x, y] = jnp.zeros(padded_im.shape[2:], BF16)
 
     barrier = pltpu.get_barrier_semaphore()
     expected = 0
@@ -265,6 +268,29 @@
     mat_copy.start()
     moduli_copy = pltpu.make_async_copy(moduli_hbm, moduli_ref, local_sems.at[2])
     moduli_copy.start()
+
+    for direction in itertools.product((-1, 0, 1), repeat=3):
+        dx, dy, dz = direction
+        if any(direction):
+            bx, by = 1 + dx, 1 + dy
+            clear = []
+            if dz:
+                clear.append(ends_rx.at[bx, by, 0 if dz < 0 else 1])
+            else:
+                x_part = {0: range(1, nx + 1), 1: (nx + 1,), -1: (0,)}[dx]
+                y_part = {0: range(1, ny + 1), 1: (ny + 1,), -1: (0,)}[dy]
+                for x, y in itertools.product(x_part, y_part):
+                    clear += [padded.at[x, y], padded_im.at[x, y]]
+                clear += [mats_rx.at[bx, by], ends_im_rx.at[bx, by]]
+
+            def wipe():
+                for ref in clear:
+                    ref[...] = jnp.zeros(ref.shape, ref.dtype)
+
+            if all(step == 0 or sizes[i] > 1 for i, step in enumerate(direction)):
+                pl.when(jnp.logical_not(exists(direction)))(wipe)
+            else:
+                wipe()
 
     vouches = max(sizes[2] - 2, 0) if direct else 0
 
@@ -315,7 +341,7 @@
         vouch(0)
 
     def gram(left, right):
-        return tree_sum([dot(left(x, y), right(x, y), 1, 1) for x, y in own])
+        return tree_sum([split_dot(*left(x, y), *right(x, y), 1, 1) for x, y in own])
 
     def sum_copy(round_, number, peer):
         axes = plans[round_][number]
@@ -323,7 +349,7 @@
         slot = offset_of(round_, number) + index
         return pltpu.make_async_remote_copy(
             src_ref=shares_of[round_].at[slot], dst_ref=shares_of[round_].at[slot],
-            send_sem=sum_send.at[round_, number], recv_sem=sum_recv.at[round_, number],
+            send_sem=sent, recv_sem=sum_recv.at[arrival(round_, number)],
             device_id=peer, device_id_type=pl.DeviceIdType.MESH,
         )
 
@@ -352,14 +378,16 @@
 
             each(count, send)
 
-    def sum_wait(round_, number, sem):
-        count, _ = group_of(plans[round_][number])
-        if count > 1:
-            part = shares_of[round_].at[pl.ds(0, count - 1)]
-            pltpu.make_async_copy(part, part, sem.at[round_, number]).wait()
+    def arrival(round_, number):
+        return sum(len(phases) for phases in plans[:round_]) + number
+
+    def sum_units(round_, number):
+        return (group_of(plans[round_][number])[0] - 1) * (2 if round_ == 1 else 1)
 
     def sum_finish(round_, number):
-        sum_wait(round_, number, sum_recv)
+        total = sum_units(round_, number)
+        if total:
+            wait_units(total, sum_recv.at[arrival(round_, number)])
         start = offset_of(round_, number)
         return tree_sum([shares_of[round_][start + peer] for peer in range(group_of(plans[round_][number])[0])])
 
@@ -370,17 +398,22 @@
     def sum_rest(round_):
         return sum_finish(round_, len(plans[round_]) - 1)
 
-    def sum_left(round_):
-        for number in range(len(plans[round_])):
-            sum_wait(round_, number, sum_send)
-
     def loads_at(x, y):
         return stack[x, y, 0:cols, :]
 
     def image_at(x, y):
         return stack[x, y, cols:, :]
 
-    square_part = gram(loads_at, loads_at)
+    for x, y in own:
+        low[x, y, 0:cols, :] = (loads_at(x, y) - padded[x + 1, y + 1].astype(F32)).astype(BF16)
+
+    def loads_split(x, y):
+        return padded[x + 1, y + 1], low[x, y, 0:cols, :]
+
+    def image_split(x, y):
+        return padded_im[x + 1, y + 1], low[x, y, cols:, :]
+
+    square_part = gram(loads_split, loads_split)
     sum_start(0, 0, pack(square_part))
     for round_ in range(1, vouches):
         vouched(round_ - 1)
@@ -405,12 +438,18 @@
         return pltpu.roll(tiles[bx, by], (2 * LANES - at - 4 * row) % LANES, 1)
 
     def modulus_of(ids):
-        return tree_sum([jnp.where(ids == float(number + 1), moduli_ref[number], 0.0) for number in range(mats)])
-
-    halo_wait(0, halo_recv.at[0])
+        found = jnp.zeros(ids.shape, F32)
+        for number in range(mats):
+            found = jnp.where(ids == float(number + 1), moduli_ref[number], found)
+        return found
+
+    own_modulus = modulus_of(mats_rx[1, 1].astype(F32))
+    halo_wait((0,), halo_recv.at[0])
     full = nz + LANES
     tails = merged(ends_rx)
-    flats = {key: modulus_of(mats_rx[key].astype(F32)) for key in tails}
+    flats = {
+        key: own_modulus if key == (1, 1) else modulus_of(mats_rx[key].astype(F32)) for key in tails
+    }
     sides = {key: modulus_of(tile[0:8]) for key, tile in tails.items()}
     moduli = {}
     for x in xs:
@@ -423,38 +462,46 @@
     for x in range(nx + 1):
         for y in range(ny + 1):
             total = (moduli[x, y] + moduli[x, y + 1]) + (moduli[x + 1, y] + moduli[x + 1, y + 1])
-            weight = 0.125 * (total + pltpu.roll(total, full - 1, 1))
-            wt[x, y] = weight
-            wtr[x, y] = pltpu.roll(weight, 1, 1)
+            after = (0.125 * k_far) * (total + pltpu.roll(total, full - 1, 1))
+            before = pltpu.roll(after, 1, 1)
+            wt[x, y], wtr[x, y], level[x, y] = after, before, before + after
+
+    def around_of(weights, x, y):
+        return (weights[x, y] + weights[x, y + 1]) + (weights[x + 1, y] + weights[x + 1, y + 1])
+
+    for x, y in own:
+        above, below = around_of(wtr, x, y), around_of(wt, x, y)
+        node[0, x, y], node[1, x, y], node[2, x, y] = above, below, (k_self / k_far) * (above + below)
 
     def double(tile):
         return jnp.concatenate([tile, tile], axis=0)
 
     def operate(direction_of, write, width=None):
         width = width or nz
+        lines, ahead_of, behind_of = {}, {}, {}
+
+        def line(x, y):
+            if (x, y) not in lines:
+                lines[x, y] = field[x, y] + field[x, y + 1]
+            return lines[x, y]
+
         for x in range(nx):
             for y in range(ny):
                 here = field[x + 1, y + 1]
-                ahead = behind = flat = None
-                w_ahead = w_behind = None
-                for ex in (x, x + 1):
-                    for ey in (y, y + 1):
-                        corner_sum = (field[ex, ey] + field[ex, ey + 1]) + (field[ex + 1, ey] + field[ex + 1, ey + 1])
-                        after, before = wt[ex, ey], wtr[ex, ey]
-                        opposite = field[2 * ex - x, 2 * ey - y][:, 0:width]
-                        one = double(before) * corner_sum
-                        two = double(after) * corner_sum
-                        three = double((before + after)[:, 0:width]) * opposite
-                        ahead = one if ahead is None else ahead + one
-                        behind = two if behind is None else behind + two
-                        flat = three if flat is None else flat + three
-                        w_ahead = before if w_ahead is None else w_ahead + before
-                        w_behind = after if w_behind is None else w_behind + after
-                ahead = ahead - double(w_ahead) * here
-                behind = behind - double(w_behind) * here
-                around = pltpu.roll(ahead, full - 1, 1)[:, 0:width] + pltpu.roll(behind, 1, 1)[:, 0:width] + flat
-                centre = double((w_ahead + w_behind)[:, 0:width]) * here[:, 0:width]
-                write(x, y, SIGMA * direction_of(x, y) + (k_far * around + k_self * centre))
+                corners = list(itertools.product((x, x + 1), (y, y + 1)))
+                flats = []
+                for ex, ey in corners:
+                    if (ex, ey) not in ahead_of:
+                        corner_sum = line(ex, ey) + line(ex + 1, ey)
+                        ahead_of[ex, ey] = double(wtr[ex, ey]) * corner_sum
+                        behind_of[ex, ey] = double(wt[ex, ey]) * corner_sum
+                    opposite = field[2 * ex - x, 2 * ey - y][:, 0:width]
+                    flats.append(double(level[ex, ey, :, 0:width]) * opposite)
+                ahead = tree_sum([ahead_of[key] for key in corners]) - double(node[0, x, y]) * here
+                behind = tree_sum([behind_of[key] for key in corners]) - double(node[1, x, y]) * here
+                around = pltpu.roll(ahead, full - 1, 1)[:, 0:width] + pltpu.roll(behind, 1, 1)[:, 0:width]
+                centre = double(node[2, x, y, :, 0:width]) * here[:, 0:width]
+                write(x, y, SIGMA * direction_of(x, y) + (around + tree_sum(flats) + centre))
 
     has_right = (me[2] < sizes[2] - 1).astype(jnp.int32)
     has_left = (me[2] > 0).astype(jnp.int32)
@@ -464,7 +511,7 @@
     def write_first(x, y, image):
         row = x * ny + y
         stack[x, y, cols:, :] = image[:, 0:nz]
-        padded_im[x + 1, y + 1] = image[:, 0:nz].astype(BF16)
+        padded_im[x + 1, y + 1], low[x, y, cols:, :] = halves(image[:, 0:nz])
         tail = jnp.where(beyond, image[:, nz:], 0.0)
         tail_im[x, y] = tail
         turned = pltpu.roll(tail, 4 * row, 1)
@@ -473,13 +520,16 @@
     operate(lambda x, y: jnp.concatenate([loads_at(x, y), field[x + 1, y + 1][:, nz:]], axis=1), write_first, full)
     ends_im[...] = image_ends[0].astype(BF16)
     halo_start(1)
-    both_part = gram(image_at, lambda x, y: stack[x, y])
+    def pair_split(x, y):
+        return jnp.concatenate([padded[x + 1, y + 1], padded_im[x + 1, y + 1]], axis=0), low[x, y]
+
+    both_part = gram(image_split, pair_split)
     if vouches:
         vouched(vouches - 1)
     sum_start(1, 0, jnp.concatenate([pack(both_part[:, 0:cols]), pack(both_part[:, cols:])], axis=0))
     sum_turn(0)
 
-    halo_wait(1, halo_recv.at[1])
+    halo_wait((1,), halo_recv.at[1])
     turned_im = {}
     for x in xs:
         for y in ys:
@@ -496,7 +546,7 @@
     last_parts = []
 
     def write_last(x, y, image):
-        last_parts.append(dot(image_at(x, y), image, 1, 1))
+        last_parts.append(split_dot(*image_split(x, y), *halves(image), 1, 1))
 
     operate(image_at, write_last)
     sum_start(2, 0, pack(tree_sum(last_parts)))
@@ -512,16 +562,16 @@
     cross, quad = unpack(table[0:half], cols), unpack(table[half:], cols)
     cross = 0.5 * (cross + cross.T)
     alpha = solve(cross, square)
-    updated = square + dot(alpha, dot(quad, alpha, 1, 0) - cross, 0, 0) - dot(cross, alpha, 0, 0)
-    grown = eye + dot(inverse, updated, 1, 0)
+    moved = dot(jnp.concatenate([quad, cross], axis=0), alpha, 1, 0)
     alpha_t = alpha.T
-    mix = jnp.concatenate([grown.T, -alpha_t], axis=1)
-    mix_hi = mix.astype(BF16)
-    mix_lo = (mix - mix_hi.astype(F32)).astype(BF16)
+    updated = square + dot(alpha_t, moved[0:cols], 1, 0) - (moved[cols:] + moved[cols:].T)
+    grown_t = eye + dot(updated, inverse, 1, 0)
+    mix = jnp.concatenate([grown_t, -alpha_t], axis=1)
+    mix_hi, mix_lo = halves(mix)
     mix_both = jnp.concatenate([mix_hi, mix_lo], axis=0)
-    known = dot(grown, dot(cross, grown, 1, 0) - dot(quad, alpha, 1, 0), 0, 0) - dot(alpha, dot(quad, grown, 1, 0), 0, 0)
-
-    known = 0.5 * (known + known.T)
+    known = dot(grown_t, dot(cross, grown_t, 1, 1), 1, 0)
+    joint = dot(grown_t, moved[0:cols], 1, 0)
+    known = 0.5 * (known + known.T) - (joint + joint.T)
 
     for x in xs:
         for y in ys:
@@ -537,38 +587,43 @@
             mixed = twice[0:cols] + twice[cols:]
             if inner:
                 direction = dot(mix, stack[x - 1, y - 1], 1, 0)
-                pair_ref[x - 1, y - 1, 0:cols, :] = direction
                 mixed = jnp.concatenate([direction, mixed], axis=1)
-            field[x, y] = mixed.astype(BF16).astype(F32)
+            rounded = mixed.astype(BF16)
+            field[x, y] = rounded.astype(F32)
+            if inner:
+                stack[x - 1, y - 1, cols:, :] = direction
+                pair_ref[x - 1, y - 1, 0, 0:cols, :] = rounded[:, 0:nz]
+                pair_ref[x - 1, y - 1, 0, cols:, :] = (direction - rounded[:, 0:nz].astype(F32)).astype(BF16)
 
     def write_second(x, y, image):
-        pair_ref[x, y, cols:, :] = image
-
-    operate(lambda x, y: pair_ref[x, y, 0:cols, :], write_second)
+        pair_ref[x, y, 1, 0:cols, :], pair_ref[x, y, 1, cols:, :] = halves(image)
+
+    operate(image_at, write_second)
+    alpha_split = halves(alpha_t)
     for x, y in own:
-        base_ref[x, y, 0:cols, :] = dot(alpha_t, stack[x, y, 0:cols, :], 1, 0)
-        base_ref[x, y, cols:, :] = stack[x, y, 0:cols, :] - dot(alpha_t, stack[x, y, cols:, :], 1, 0)
-    halo_wait(0, halo_send.at[0])
-    halo_wait(1, halo_send.at[1])
-    sum_left(0)
-    sum_left(1)
+        base_ref[x, y, 0:cols, :] = split_dot(*alpha_split, *loads_split(x, y), 1, 0)
+        base_ref[x, y, cols:, :] = loads_at(x, y) - split_dot(*alpha_split, *image_split(x, y), 1, 0)
+    halo_wait((0, 1), sent, sum(
+        sum_units(round_, number) for round_ in range(3) for number in range(len(plans[round_]))
+        if (round_, number) != (2, 1)
+    ))
     sum_turn(2)
     last = unpack(sum_rest(2), cols)
     turned = dot(alpha_t, last, 1, 0) + dot(alpha_t, last, 1, 1)
-    coef_ref[...] = solve(known + 0.5 * dot(turned, alpha, 1, 0), updated).T
-    sum_left(2)
+    coef_ref[0:cols, :], coef_ref[cols:, :] = halves(solve(known + 0.5 * dot(turned, alpha, 1, 0), updated).T)
+    if len(plans[2]) > 1:
+        wait_units(sum_units(2, 1), sent)
 
 
 def last_body(coef_ref, base_ref, pair_ref, sol_ref, res_ref, stage, sems):
     cols, nx, ny, nz = sol_ref.shape
-    coef = coef_ref[...]
+    high, low = coef_ref[0:cols, :], coef_ref[cols:, :]
     for x in range(nx):
         for which, ref, sign in ((0, sol_ref, 1.0), (1, res_ref, -1.0)):
             rows = slice(which * cols, (which + 1) * cols)
             for y in range(ny):
-                stage[which, :, x, y, :] = (
-                    base_ref[x, y, rows, :] + sign * dot(coef, pair_ref[x, y, rows, :], 1, 0)
-                )
+                added = split_dot(high, low, pair_ref[x, y, which, 0:cols, :], pair_ref[x, y, which, cols:, :], 1, 0)
+                stage[which, :, x, y, :] = base_ref[x, y, rows, :] + sign * added
             pltpu.make_async_copy(stage.at[which, :, x], ref.at[:, x], sems.at[which]).start()
     for which in range(2):
         pltpu.make_async_copy(stage.at[which], stage.at[which], sems.at[which]).wait()
@@ -587,18 +642,20 @@
     vmem = pl.BlockSpec(memory_space=pltpu.VMEM)
     anywhere = pl.BlockSpec(memory_space=pl.ANY)
     full = nz + LANES
-    credits = (nz // LANES) * 2 * (nx + ny + 2) + 18 + 8 * (nx * ny * nz // (cols * LANES))
+    tiles = 2 * ((nz // LANES) * 2 * (nx + ny + 2) + 26) + 8 * (nx * ny * nz // (cols * LANES))
+    credits = tiles * TILE_UNITS // cols + 2 * sum(slots(phases) for phases in plans)
     base, pair, coef = pl.pallas_call(
         functools.partial(main_body, sizes, plans, stiffness_values()),
         out_shape=(
             pltpu.VMEM((nx, ny, 2 * cols, nz), F32),
-            pltpu.VMEM((nx, ny, 2 * cols, nz), F32),
-            pltpu.VMEM((cols, cols), F32),
+            pltpu.VMEM((nx, ny, 2, 2 * cols, nz), BF16),
+            pltpu.VMEM((2 * cols, cols), BF16),
         ),
         in_specs=[anywhere, anywhere, anywhere],
         out_specs=(vmem, vmem, vmem),
         scratch_shapes=[
             pltpu.VMEM((nx, ny, 2 * cols, nz), F32),
+            pltpu.VMEM((nx, ny, 2 * cols, nz), BF16),
             pltpu.VMEM((nx + 2, ny + 2, cols, nz), BF16),
             pltpu.VMEM((nx + 2, ny + 2, cols, nz), BF16),
             pltpu.VMEM((3, 3, nx * ny, nz), BF16),
@@ -609,17 +666,18 @@
             pltpu.VMEM((nx + 2, ny + 2, cols, full), F32),
             pltpu.VMEM((nx + 1, ny + 1, 8, full), F32),
             pltpu.VMEM((nx + 1, ny + 1, 8, full), F32),
+            pltpu.VMEM((nx + 1, ny + 1, 8, full), F32),
+            pltpu.VMEM((3, nx, ny, 8, full), F32),
             pltpu.VMEM((slots(plans[0]), cols * cols // LANES, LANES), F32),
             pltpu.VMEM((slots(plans[1]), 2 * cols * cols // LANES, LANES), F32),
             pltpu.VMEM((slots(plans[2]), cols * cols // LANES, LANES), F32),
             pltpu.VMEM((nx, ny, cols, LANES), F32),
             pltpu.SMEM(moduli.shape, F32),
             pltpu.VMEM(material.shape, jnp.int32),
-            pltpu.VMEM((credits, cols, LANES), BF16),
+            pltpu.VMEM((credits, cols * cols // LANES, LANES), F32),
+            pltpu.SemaphoreType.DMA,
             pltpu.SemaphoreType.DMA((2,)),
-            pltpu.SemaphoreType.DMA((2,)),
-            pltpu.SemaphoreType.DMA((3, 2)),
-            pltpu.SemaphoreType.DMA((3, 2)),
+            pltpu.SemaphoreType.DMA((sum(len(phases) for phases in plans),)),
             pltpu.SemaphoreType.DMA((3,)),
             pltpu.SemaphoreType.REGULAR((max(sizes[2] - 2, 1) if count <= DIRECT_LIMIT else 1, 2)),
         ],

time: 20.7 us -> 20.2 us (0.976)
  Pallas kernels: 19.9 us -> 19.4 us
    pallas_call x1, Pallas kernels: 18.8 us -> 18.4 us  [on_device(): pl.pallas_call(functools.partial(main_body, sizes, plans, stiffness_value...]
where the time goes in v3:
time: 20.2 us; the launch traced here: 20 us
  Pallas kernels  19.4 us (96%)
  between operations  0.64 us (3%)
    pallas_call x1, Pallas kernels, on_device(): pl.pallas_call(functools.partial(main_body, sizes, plans, stiffness_value...  18.4 us
    pallas_call x1, Pallas kernels, on_device(): pl.pallas_call(last_body, out_shape=(out, out), in_specs=[vmem, vmem, vme...  0.92 us

profile of v3, /device:TPU:0, one launch (start us, length us, event | category | flops | bytes accessed | tf_op | source)
XLA Modules:
  0.0 20.0 jit_solution(11159079690146511023)
XLA Ops:
  0.6 18.4 %shard_map.50 = (f32[2,4,32,256]{3,2,1,0:T(8,128)S(1)}, bf16[2,4,2,32,256]{4,3,2,1,0:T(8,128)(2,1)S(1)}, bf16[32,16]{1,0:T(8,128)(2,1)S(1)}) custom-call(f32[8]{0:T(128)} %moduli_hbm.1, f32[16,2,4,256]{3,2,1,0:T(4,128)} %loads_ref.1, s32[2,4,256]{2,1,0:T(4,128)} %mat_hbm.1), custom_call_target="tpu_custom_call" | custom-call | tf_op jit(solution)/shard_map/pallas_call | solution.py:647
  19.1 0.9 %shard_map.51 = (f32[16,2,4,256]{3,2,1,0:T(4,128)}, f32[16,2,4,256]{3,2,1,0:T(4,128)}) custom-call(bf16[32,16]{1,0:T(8,128)(2,1)S(1)} %get-tuple-element.5.coef_ref, f32[2,4,32,256]{3,2,1,0:T(8,128)S(1)} %get-tuple-element.6.base_ref, bf16[2,4,2,32,256]{4,3,2,1,0:T(8,128)(2,1)S(1)} %get-tuple-element.7.pair_ref), custom_call_target="tpu_custom_call" | custom-call | tf_op jit(solution)/shard_map/pallas_call | solution.py:687

commit v4 on v3

--- a/solution.py
+++ b/solution.py
@@ -16,7 +16,7 @@
 BF16 = jnp.bfloat16
 LANES = 128
 DIRECT_LIMIT = 32
-IDS = 64
+IDS = 32
 TILE_UNITS = 64
 
 
@@ -58,29 +58,52 @@
     turned = [tall] + [pltpu.roll(tall, LANES - cols * group, 1) for group in range(1, 8)]
     return jnp.concatenate(
         [turned[group][row : row + 1] for row in range(rows) for group in range(8)], axis=0
-    )[:, 0:cols]
-
-
-def solve(matrix, rhs):
-    size = matrix.shape[0]
-    wide = jnp.concatenate([rhs, jnp.zeros((size, LANES - rhs.shape[1]), F32)], axis=1)
-    left = [jnp.broadcast_to(matrix[:, i : i + 1], (size, LANES)) for i in range(size)]
-    right = [wide[i : i + 1, :] for i in range(size)]
+    )
+
+
+def solve(columns, right):
+    size = len(right)
+    scales = [1.0 / columns[i][i : i + 1, :] for i in range(size)]
+    left = [columns[i] * scales[i] for i in range(size)]
+    right = [right[i] * scales[i] for i in range(size)]
     start = 0
-    for step in range(size):
+    for step in range(0, size, 2):
         if step == size // 2 and step % 8 == 0:
             left = [row[step:, :] for row in left]
             start = step
         at = step - start
-        scale = 1.0 / left[step][at : at + 1, :]
-        pivot, pivot_right = left[step] * scale, right[step] * scale
+        top, low, top_right, low_right = left[step], left[step + 1], right[step], right[step + 1]
+        first, mixed = top[at : at + 1, :], top[at + 1 : at + 2, :]
+        cross, second = low[at : at + 1, :], low[at + 1 : at + 2, :]
+        scale = 1.0 / (first * second - mixed * cross)
+        aa, ab, ba, bb = second * scale, mixed * scale, cross * scale, first * scale
+        one, two = aa * top - ab * low, bb * low - ba * top
+        one_right, two_right = aa * top_right - ab * low_right, bb * low_right - ba * top_right
         for i in range(size):
-            if i != step:
-                factor = left[i][at : at + 1, :]
-                left[i] = left[i] - factor * pivot
-                right[i] = right[i] - factor * pivot_right
-        left[step], right[step] = pivot, pivot_right
-    return jnp.concatenate(right, axis=0)[:, 0 : rhs.shape[1]]
+            if i not in (step, step + 1):
+                factor, other = left[i][at : at + 1, :], left[i][at + 1 : at + 2, :]
+                left[i] = left[i] - (factor * one + other * two)
+                right[i] = right[i] - (factor * one_right + other * two_right)
+        left[step], left[step + 1], right[step], right[step + 1] = one, two, one_right, two_right
+    return right
+
+
+def columns_of(matrix):
+    size = matrix.shape[0]
+    return [jnp.broadcast_to(matrix[:, k : k + 1], (size, LANES)) for k in range(size)]
+
+
+def rows_of(matrix):
+    return [matrix[k : k + 1, :] for k in range(matrix.shape[0])]
+
+
+def weave(columns, rows):
+    return tree_sum([column * row for column, row in zip(columns, rows)])
+
+
+def turn(matrix):
+    size = matrix.shape[0]
+    return jnp.concatenate([matrix[:, 0:size].T, jnp.zeros((size, LANES - size), F32)], axis=1)
 
 
 def halves(value):
@@ -101,16 +124,16 @@
 
 
 def main_body(sizes, plans, stiff, moduli_hbm, loads_ref, mat_hbm, base_ref, pair_ref, coef_ref,
-              stack, low, padded, padded_im, mats_rx, ends, ends_rx, ends_im, ends_im_rx, field, wt, wtr, level, node,
-              shares_square, shares_table, shares_last, tail_im, moduli_ref, mat_ref, credit,
-              sent, halo_recv, sum_recv, local_sems, vouch_sem):
+              stack, low, padded, padded_im, mats_rx, ends, ends_rx, field, field_im, wt, wtr, level, node,
+              shares_square, shares_table, shares_last, moduli_ref, mat_ref, credit,
+              sent, sent_first, halo_recv, sum_recv, local_sems, vouch_sem):
     cols, nx, ny, nz = loads_ref.shape
     mats = moduli_ref.shape[0]
     me = [lax.axis_index(axis) for axis in AXES]
     k_self, k_edge, k_far = stiff[0], stiff[1], stiff[2]
     assert k_edge == 0.0 and stiff[2] == stiff[3]
     assert 4 * nx * ny <= IDS and (nx * ny * nz) % (cols * LANES) == 0 and nz % LANES == 0 and TILE_UNITS % cols == 0
-    xs, ys = range(nx + 2), range(ny + 2)
+    assert nx >= 2 and ny >= 2
     shares_of = (shares_square, shares_table, shares_last)
     own = list(itertools.product(range(nx), range(ny)))
 
@@ -134,21 +157,33 @@
     def place(direction):
         return 1 - direction[0], 1 - direction[1]
 
+    def spans(step, size, ring):
+        if step == 0:
+            return pl.ds(2, size), pl.ds(2, size)
+        if ring == 0:
+            return (pl.ds(size, 2), pl.ds(0, 2)) if step > 0 else (pl.ds(2, 2), pl.ds(size + 2, 2))
+        if step > 0:
+            return pl.ds(size + 2 - ring, 1), pl.ds(2 - ring, 1)
+        return pl.ds(1 + ring, 1), pl.ds(size + 1 + ring, 1)
+
+    def slab(direction, ring_x, ring_y):
+        src_x, dst_x = spans(direction[0], nx, ring_x)
+        src_y, dst_y = spans(direction[1], ny, ring_y)
+        return padded.at[src_x, src_y], padded.at[dst_x, dst_y]
+
     def halo_start(round_):
-        core = (padded, padded_im)[round_]
         for direction in directions:
             dx, dy, dz = direction
             pairs = []
             if dz == 0:
-                src_x = {0: pl.ds(1, nx), 1: pl.ds(nx, 1), -1: pl.ds(1, 1)}[dx]
-                dst_x = {0: pl.ds(1, nx), 1: pl.ds(0, 1), -1: pl.ds(nx + 1, 1)}[dx]
-                src_y = {0: pl.ds(1, ny), 1: pl.ds(ny, 1), -1: pl.ds(1, 1)}[dy]
-                dst_y = {0: pl.ds(1, ny), 1: pl.ds(0, 1), -1: pl.ds(ny + 1, 1)}[dy]
-                pairs.append((core.at[src_x, src_y], core.at[dst_x, dst_y]))
                 if round_ == 0:
+                    pairs.append(slab(direction, 1, 1))
                     pairs.append((mats_rx.at[1, 1], mats_rx.at[place(direction)]))
+                elif dx and dy:
+                    pairs.append(slab(direction, 2, 0))
+                    pairs.append(slab(direction, 1, 2))
                 else:
-                    pairs.insert(0, (ends_im, ends_im_rx.at[place(direction)]))
+                    pairs.append(slab(direction, 2, 2))
             elif round_ == 0:
                 pairs.append((ends.at[1 if dz > 0 else 0], ends_rx.at[(*place(direction), 0 if dz > 0 else 1)]))
             else:
@@ -158,7 +193,7 @@
             def _():
                 for src, dst in pairs:
                     pltpu.make_async_remote_copy(
-                        src_ref=src, dst_ref=dst, send_sem=sent, recv_sem=halo_recv.at[round_],
+                        src_ref=src, dst_ref=dst, send_sem=sent if round_ else sent_first, recv_sem=halo_recv.at[round_],
                         device_id=target(direction), device_id_type=pl.DeviceIdType.MESH,
                     ).start()
 
@@ -173,14 +208,13 @@
         choices = [(0,) if size == 1 else (1,) if size == 2 else (1, 2) for size in sizes]
         per = nz // LANES
         for cx, cy, cz in itertools.product(*choices):
-            total = 0
+            total, more_units = 0, more
             for round_ in rounds:
-                total += per * (cx * ny + cy * nx + cx * cy)
+                total += per * (cx * ny + cy * nx + (1 if round_ == 0 else 3) * cx * cy)
                 if round_ == 0:
-                    total += (cx + cy + cx * cy) * (nx * ny * nz // (cols * LANES)) + cz * (1 + cx) * (1 + cy)
-                else:
-                    total += cx + cy + cx * cy
-            total = total * TILE_UNITS // cols + more
+                    total += (cx + cy + cx * cy) * (nx * ny * nz // (cols * LANES))
+                    more_units += cz * (1 + cx) * (1 + cy) * TILE_UNITS // cols // 2
+            total = total * TILE_UNITS // cols + more_units
             if total:
                 tests = [numbers[i] == c for i, c in enumerate((cx, cy, cz)) if len(choices[i]) > 1]
                 take = functools.partial(wait_units, total, sem)
@@ -277,11 +311,11 @@
             if dz:
                 clear.append(ends_rx.at[bx, by, 0 if dz < 0 else 1])
             else:
-                x_part = {0: range(1, nx + 1), 1: (nx + 1,), -1: (0,)}[dx]
-                y_part = {0: range(1, ny + 1), 1: (ny + 1,), -1: (0,)}[dy]
+                x_part = {0: range(2, nx + 2), 1: (nx + 2, nx + 3), -1: (0, 1)}[dx]
+                y_part = {0: range(2, ny + 2), 1: (ny + 2, ny + 3), -1: (0, 1)}[dy]
                 for x, y in itertools.product(x_part, y_part):
-                    clear += [padded.at[x, y], padded_im.at[x, y]]
-                clear += [mats_rx.at[bx, by], ends_im_rx.at[bx, by]]
+                    clear.append(padded.at[x, y])
+                clear.append(mats_rx.at[bx, by])
 
             def wipe():
                 for ref in clear:
@@ -331,10 +365,12 @@
     pltpu.make_async_copy(whole, whole, local_sems.at[0]).wait()
     for x, y in own:
         values = stack[x, y, 0:cols, :]
-        padded[x + 1, y + 1] = values.astype(BF16)
+        padded[x + 2, y + 2] = values.astype(BF16)
         firsts, lasts = spread(firsts, lasts, x * ny + y, values[:, 0:LANES], values[:, nz - LANES : nz], 0)
-    ends[0] = firsts.astype(BF16)
-    ends[1] = lasts.astype(BF16)
+    upper = cols // 2
+    for side, tile in enumerate((firsts, lasts)):
+        lower_half = jnp.logical_and(lane >= 2 * LANES // 4 - 2, lane < LANES - 2)
+        ends[side] = jnp.where(lower_half, pltpu.roll(tile[upper:], LANES // 2, 1), tile[0:upper]).astype(BF16)
     pl.semaphore_wait(barrier, expected)
     halo_start(0)
     if vouches:
@@ -405,24 +441,26 @@
         return stack[x, y, cols:, :]
 
     for x, y in own:
-        low[x, y, 0:cols, :] = (loads_at(x, y) - padded[x + 1, y + 1].astype(F32)).astype(BF16)
+        low[x, y, 0:cols, :] = (loads_at(x, y) - padded[x + 2, y + 2].astype(F32)).astype(BF16)
 
     def loads_split(x, y):
-        return padded[x + 1, y + 1], low[x, y, 0:cols, :]
+        return padded[x + 2, y + 2], low[x, y, 0:cols, :]
 
     def image_split(x, y):
-        return padded_im[x + 1, y + 1], low[x, y, cols:, :]
+        return padded_im[x, y], low[x, y, cols:, :]
 
     square_part = gram(loads_split, loads_split)
     sum_start(0, 0, pack(square_part))
     for round_ in range(1, vouches):
         vouched(round_ - 1)
         vouch(round_)
+    halo_wait((0,), sent_first)
+    halo_start(1)
     moduli_copy.wait()
 
     def block_of(x, y):
-        bx, lx = (0, nx - 1) if x == 0 else (2, 0) if x == nx + 1 else (1, x - 1)
-        by, ly = (0, ny - 1) if y == 0 else (2, 0) if y == ny + 1 else (1, y - 1)
+        bx, lx = (0, nx - 2 + x) if x < 2 else (2, x - nx - 2) if x >= nx + 2 else (1, x - 2)
+        by, ly = (0, ny - 2 + y) if y < 2 else (2, y - ny - 2) if y >= ny + 2 else (1, y - 2)
         return bx, by, lx * ny + ly
 
     odd = lax.rem(lane, 4) >= 2
@@ -435,7 +473,11 @@
 
     def tail_of(tiles, x, y, at=0):
         bx, by, row = block_of(x, y)
-        return pltpu.roll(tiles[bx, by], (2 * LANES - at - 4 * row) % LANES, 1)
+        tile = tiles[bx, by]
+        near, far = ((2 * LANES - spot - 4 * row) % LANES for spot in (at, at + LANES // 2))
+        if at:
+            return pltpu.roll(tile, near, 1)
+        return jnp.concatenate([pltpu.roll(tile, near, 1), pltpu.roll(tile, far, 1)], axis=0)
 
     def modulus_of(ids):
         found = jnp.zeros(ids.shape, F32)
@@ -445,172 +487,196 @@
 
     own_modulus = modulus_of(mats_rx[1, 1].astype(F32))
     halo_wait((0,), halo_recv.at[0])
+    if vouches:
+        vouched(vouches - 1)
+    sum_turn(0)
     full = nz + LANES
     tails = merged(ends_rx)
     flats = {
         key: own_modulus if key == (1, 1) else modulus_of(mats_rx[key].astype(F32)) for key in tails
     }
-    sides = {key: modulus_of(tile[0:8]) for key, tile in tails.items()}
+    sides = {key: modulus_of(tile) for key, tile in tails.items()}
     moduli = {}
-    for x in xs:
-        for y in ys:
-            field[x, y] = jnp.concatenate([padded[x, y].astype(F32), tail_of(tails, x, y)], axis=1)
+
+    def modulus_at(x, y):
+        if (x, y) not in moduli:
             bx, by, row = block_of(x, y)
             moduli[x, y] = jnp.concatenate([
                 jnp.broadcast_to(flats[bx, by][row : row + 1, :], (8, nz)), tail_of(sides, x, y, IDS)
             ], axis=1)
-    for x in range(nx + 1):
-        for y in range(ny + 1):
-            total = (moduli[x, y] + moduli[x, y + 1]) + (moduli[x + 1, y] + moduli[x + 1, y + 1])
-            after = (0.125 * k_far) * (total + pltpu.roll(total, full - 1, 1))
-            before = pltpu.roll(after, 1, 1)
-            wt[x, y], wtr[x, y], level[x, y] = after, before, before + after
+        return moduli[x, y]
+
+    def weigh(x, y):
+        total = (modulus_at(x, y) + modulus_at(x, y + 1)) + (modulus_at(x + 1, y) + modulus_at(x + 1, y + 1))
+        total = (0.125 * k_far) * total
+        after, before = total + pltpu.roll(total, full - 1, 1), total + pltpu.roll(total, 1, 1)
+        wt[x, y], wtr[x, y], level[x, y] = after, before, before + after
 
     def around_of(weights, x, y):
         return (weights[x, y] + weights[x, y + 1]) + (weights[x + 1, y] + weights[x + 1, y + 1])
 
-    for x, y in own:
+    def gather(x, y):
         above, below = around_of(wtr, x, y), around_of(wt, x, y)
         node[0, x, y], node[1, x, y], node[2, x, y] = above, below, (k_self / k_far) * (above + below)
 
+    def unfold(x, y):
+        field[x, y] = jnp.concatenate([padded[x, y].astype(F32), tail_of(tails, x, y)], axis=1)
+
+    inner = list(itertools.product(range(1, nx + 1), range(1, ny + 1)))
+    outer = [key for key in itertools.product(range(nx + 2), range(ny + 2)) if key not in inner]
+    near = list(itertools.product(range(1, nx + 3), range(1, ny + 3)))
+    near_elements = list(itertools.product(range(1, nx + 2), range(1, ny + 2)))
+    for key in near:
+        unfold(*key)
+    for key in near_elements:
+        weigh(*key)
+    for key in inner:
+        gather(*key)
+
     def double(tile):
         return jnp.concatenate([tile, tile], axis=0)
 
-    def operate(direction_of, write, width=None):
-        width = width or nz
+    def operate(source, shift, cells, direction_of, write, width):
         lines, ahead_of, behind_of = {}, {}, {}
 
         def line(x, y):
             if (x, y) not in lines:
-                lines[x, y] = field[x, y] + field[x, y + 1]
+                lines[x, y] = source[x - shift, y - shift] + source[x - shift, y + 1 - shift]
             return lines[x, y]
 
-        for x in range(nx):
-            for y in range(ny):
-                here = field[x + 1, y + 1]
-                corners = list(itertools.product((x, x + 1), (y, y + 1)))
-                flats = []
-                for ex, ey in corners:
-                    if (ex, ey) not in ahead_of:
-                        corner_sum = line(ex, ey) + line(ex + 1, ey)
-                        ahead_of[ex, ey] = double(wtr[ex, ey]) * corner_sum
-                        behind_of[ex, ey] = double(wt[ex, ey]) * corner_sum
-                    opposite = field[2 * ex - x, 2 * ey - y][:, 0:width]
-                    flats.append(double(level[ex, ey, :, 0:width]) * opposite)
-                ahead = tree_sum([ahead_of[key] for key in corners]) - double(node[0, x, y]) * here
-                behind = tree_sum([behind_of[key] for key in corners]) - double(node[1, x, y]) * here
-                around = pltpu.roll(ahead, full - 1, 1)[:, 0:width] + pltpu.roll(behind, 1, 1)[:, 0:width]
-                centre = double(node[2, x, y, :, 0:width]) * here[:, 0:width]
-                write(x, y, SIGMA * direction_of(x, y) + (around + tree_sum(flats) + centre))
+        for x, y in cells:
+            here = source[x + 1 - shift, y + 1 - shift]
+            corners = list(itertools.product((x, x + 1), (y, y + 1)))
+            flats = []
+            for ex, ey in corners:
+                if (ex, ey) not in ahead_of:
+                    corner_sum = line(ex, ey) + line(ex + 1, ey)
+                    ahead_of[ex, ey] = double(wtr[ex, ey]) * corner_sum
+                    behind_of[ex, ey] = double(wt[ex, ey]) * corner_sum
+                opposite = source[2 * ex - x - shift, 2 * ey - y - shift][:, 0:width]
+                flats.append(double(level[ex, ey, :, 0:width]) * opposite)
+            ahead = tree_sum([ahead_of[key] for key in corners]) - double(node[0, x, y]) * here
+            behind = tree_sum([behind_of[key] for key in corners]) - double(node[1, x, y]) * here
+            around = pltpu.roll(ahead, full - 1, 1)[:, 0:width] + pltpu.roll(behind, 1, 1)[:, 0:width]
+            centre = double(node[2, x, y, :, 0:width]) * here[:, 0:width]
+            write(x, y, SIGMA * direction_of(x, y) + (around + tree_sum(flats) + centre))
 
     has_right = (me[2] < sizes[2] - 1).astype(jnp.int32)
     has_left = (me[2] > 0).astype(jnp.int32)
     beyond = jnp.logical_or(lane < has_right, lane >= LANES - has_left)
-    image_ends = [jnp.zeros((cols, LANES), F32)]
 
     def write_first(x, y, image):
-        row = x * ny + y
-        stack[x, y, cols:, :] = image[:, 0:nz]
-        padded_im[x + 1, y + 1], low[x, y, cols:, :] = halves(image[:, 0:nz])
-        tail = jnp.where(beyond, image[:, nz:], 0.0)
-        tail_im[x, y] = tail
-        turned = pltpu.roll(tail, 4 * row, 1)
-        image_ends[0] = image_ends[0] + turned
-
-    operate(lambda x, y: jnp.concatenate([loads_at(x, y), field[x + 1, y + 1][:, nz:]], axis=1), write_first, full)
-    ends_im[...] = image_ends[0].astype(BF16)
-    halo_start(1)
+        main = image[:, 0:nz]
+        stack[x - 1, y - 1, cols:, :] = main
+        padded_im[x - 1, y - 1], low[x - 1, y - 1, cols:, :] = halves(main)
+        field_im[x, y] = jnp.concatenate([main, jnp.where(beyond, image[:, nz:], 0.0)], axis=1)
+
+    def loads_wide(x, y):
+        return jnp.concatenate([loads_at(x - 1, y - 1), field[x + 1, y + 1][:, nz:]], axis=1)
+
+    operate(field, 0, inner, loads_wide, write_first, full)
+
     def pair_split(x, y):
-        return jnp.concatenate([padded[x + 1, y + 1], padded_im[x + 1, y + 1]], axis=0), low[x, y]
+        return jnp.concatenate([padded[x + 2, y + 2], padded_im[x, y]], axis=0), low[x, y]
 
     both_part = gram(image_split, pair_split)
-    if vouches:
-        vouched(vouches - 1)
     sum_start(1, 0, jnp.concatenate([pack(both_part[:, 0:cols]), pack(both_part[:, cols:])], axis=0))
-    sum_turn(0)
-
+    for key in itertools.product(range(nx + 3), range(ny + 3)):
+        if key not in near_elements:
+            weigh(*key)
+    for key in outer:
+        gather(*key)
     halo_wait((1,), halo_recv.at[1])
-    turned_im = {}
-    for x in xs:
-        for y in ys:
-            if 1 <= x <= nx and 1 <= y <= ny:
-                turned_im[x, y] = tail_im[x - 1, y - 1]
-            else:
-                bx, by, row = block_of(x, y)
-                turned_im[x, y] = pltpu.roll(ends_im_rx[bx, by].astype(F32), (LANES - 4 * row) % LANES, 1)
-    for x in xs:
-        for y in ys:
-            inner = 1 <= x <= nx and 1 <= y <= ny
-            value = image_at(x - 1, y - 1) if inner else padded_im[x, y].astype(F32)
-            field[x, y] = jnp.concatenate([value, turned_im[x, y]], axis=1)
+    for key in itertools.product(range(nx + 4), range(ny + 4)):
+        if key not in near:
+            unfold(*key)
+
+    def write_ring(x, y, image):
+        dx = -1 if x == 0 else 1 if x == nx + 1 else 0
+        dy = -1 if y == 0 else 1 if y == ny + 1 else 0
+        if any(step and sizes[i] == 1 for i, step in enumerate((dx, dy))):
+            field_im[x, y] = jnp.zeros(image.shape, F32)
+        else:
+            image = jnp.where(exists((dx, dy, 0)), image, 0.0)
+            field_im[x, y] = jnp.concatenate([image[:, 0:nz], jnp.where(beyond, image[:, nz:], 0.0)], axis=1)
+
+    operate(field, 0, outer, lambda x, y: field[x + 1, y + 1], write_ring, full)
     last_parts = []
 
     def write_last(x, y, image):
-        last_parts.append(split_dot(*image_split(x, y), *halves(image), 1, 1))
-
-    operate(image_at, write_last)
+        last_parts.append(split_dot(*image_split(x - 1, y - 1), *halves(image), 1, 1))
+
+    operate(field_im, 1, inner, lambda x, y: image_at(x - 1, y - 1), write_last, nz)
     sum_start(2, 0, pack(tree_sum(last_parts)))
 
     square = unpack(sum_rest(0), cols)
     sum_turn(1)
-    row_id = lax.broadcasted_iota(jnp.int32, (cols, cols), 0)
-    col_id = lax.broadcasted_iota(jnp.int32, (cols, cols), 1)
+    row_id = lax.broadcasted_iota(jnp.int32, (cols, LANES), 0)
+    col_id = lax.broadcasted_iota(jnp.int32, (cols, LANES), 1)
     eye = jnp.where(row_id == col_id, 1.0, 0.0)
-    inverse = solve(square, eye)
+    inverse = solve(columns_of(square), rows_of(eye))
     table = sum_rest(1)
     half = table.shape[0] // 2
     cross, quad = unpack(table[0:half], cols), unpack(table[half:], cols)
-    cross = 0.5 * (cross + cross.T)
-    alpha = solve(cross, square)
-    moved = dot(jnp.concatenate([quad, cross], axis=0), alpha, 1, 0)
-    alpha_t = alpha.T
-    updated = square + dot(alpha_t, moved[0:cols], 1, 0) - (moved[cols:] + moved[cols:].T)
-    grown_t = eye + dot(updated, inverse, 1, 0)
-    mix = jnp.concatenate([grown_t, -alpha_t], axis=1)
-    mix_hi, mix_lo = halves(mix)
-    mix_both = jnp.concatenate([mix_hi, mix_lo], axis=0)
-    known = dot(grown_t, dot(cross, grown_t, 1, 1), 1, 0)
-    joint = dot(grown_t, moved[0:cols], 1, 0)
-    known = 0.5 * (known + known.T) - (joint + joint.T)
-
-    for x in xs:
-        for y in ys:
-            inner = 1 <= x <= nx and 1 <= y <= ny
-            near_tail = jnp.concatenate([
-                tail_of(tails, x, y).astype(BF16), turned_im[x, y].astype(BF16)
-            ], axis=0)
-            if not inner:
-                near_tail = jnp.concatenate([
-                    jnp.concatenate([padded[x, y], padded_im[x, y]], axis=0), near_tail
-                ], axis=1)
-            twice = dot(mix_both, near_tail, 1, 0, None)
-            mixed = twice[0:cols] + twice[cols:]
-            if inner:
-                direction = dot(mix, stack[x - 1, y - 1], 1, 0)
-                mixed = jnp.concatenate([direction, mixed], axis=1)
-            rounded = mixed.astype(BF16)
-            field[x, y] = rounded.astype(F32)
-            if inner:
-                stack[x - 1, y - 1, cols:, :] = direction
-                pair_ref[x - 1, y - 1, 0, 0:cols, :] = rounded[:, 0:nz]
-                pair_ref[x - 1, y - 1, 0, cols:, :] = (direction - rounded[:, 0:nz].astype(F32)).astype(BF16)
-
-    def write_second(x, y, image):
-        pair_ref[x, y, 1, 0:cols, :], pair_ref[x, y, 1, cols:, :] = halves(image)
-
-    operate(image_at, write_second)
+    cross = 0.5 * (cross + turn(cross))
+    cross_columns = columns_of(cross)
+    alpha_rows = solve(cross_columns, rows_of(square))
+    alpha_t = turn(jnp.concatenate(alpha_rows, axis=0))
+    alpha_columns = columns_of(alpha_t)
+    moved, stood = weave(columns_of(quad), alpha_rows), weave(cross_columns, alpha_rows)
+    alpha_t = alpha_t[:, 0:cols]
     alpha_split = halves(alpha_t)
-    for x, y in own:
-        base_ref[x, y, 0:cols, :] = split_dot(*alpha_split, *loads_split(x, y), 1, 0)
-        base_ref[x, y, cols:, :] = loads_at(x, y) - split_dot(*alpha_split, *image_split(x, y), 1, 0)
-    halo_wait((0, 1), sent, sum(
+    alpha_both = jnp.concatenate(alpha_split, axis=0)
+    cells = list(itertools.product(range(nx + 2), range(ny + 2)))
+
+    def start_of(cell):
+        return nz if cell in inner else 0
+
+    for x, y in cells:
+        start = start_of((x, y))
+        twice = dot(alpha_both, field_im[x, y, :, start:].astype(BF16), 1, 0, None)
+        field_im[x, y, :, start:] = field[x + 1, y + 1, :, start:] - (twice[0:cols] + twice[cols:])
+        if (x, y) in inner:
+            base_ref[x - 1, y - 1, cols:, :] = loads_at(x - 1, y - 1) - dot(alpha_t, image_at(x - 1, y - 1), 1, 0)
+    updated = square + weave(alpha_columns, rows_of(moved)) - (stood + turn(stood))
+    beta_t = weave(columns_of(updated), inverse)
+    grown_t = eye + beta_t
+    grown_columns = columns_of(grown_t)
+    joint = weave(grown_columns, rows_of(moved))
+    known = weave(columns_of(weave(grown_columns, rows_of(cross))), rows_of(turn(grown_t))) - (joint + turn(joint))
+    beta_t = beta_t[:, 0:cols]
+    beta_both = jnp.concatenate(halves(beta_t), axis=0)
+    for x, y in cells:
+        start = start_of((x, y))
+        twice = dot(beta_both, field[x + 1, y + 1, :, start:].astype(BF16), 1, 0, None)
+        mixed = field_im[x, y, :, start:] + (twice[0:cols] + twice[cols:])
+        if (x, y) in inner:
+            direction = base_ref[x - 1, y - 1, cols:, :] + dot(beta_t, loads_at(x - 1, y - 1), 1, 0)
+            mixed = jnp.concatenate([direction, mixed], axis=1)
+        rounded = mixed.astype(BF16)
+        field_im[x, y] = rounded.astype(F32)
+        if (x, y) in inner:
+            stack[x - 1, y - 1, cols:, :] = direction
+            pair_ref[x - 1, y - 1, 0, 0:cols, :] = rounded[:, 0:nz]
+            pair_ref[x - 1, y - 1, 0, cols:, :] = (direction - rounded[:, 0:nz].astype(F32)).astype(BF16)
+
+    halo_wait((1,), sent, sum(
         sum_units(round_, number) for round_ in range(3) for number in range(len(plans[round_]))
         if (round_, number) != (2, 1)
     ))
     sum_turn(2)
     last = unpack(sum_rest(2), cols)
-    turned = dot(alpha_t, last, 1, 0) + dot(alpha_t, last, 1, 1)
-    coef_ref[0:cols, :], coef_ref[cols:, :] = halves(solve(known + 0.5 * dot(turned, alpha, 1, 0), updated).T)
+    total = known + weave(alpha_columns, rows_of(weave(columns_of(last), alpha_rows)))
+    last_rows = solve(columns_of(total), rows_of(updated))
+    coef_t = jnp.concatenate(last_rows, axis=0)[:, 0:cols].T
+    coef_ref[0:cols, :], coef_ref[cols:, :] = halves(coef_t)
+
+    def write_second(x, y, image):
+        pair_ref[x - 1, y - 1, 1, 0:cols, :], pair_ref[x - 1, y - 1, 1, cols:, :] = halves(image)
+
+    operate(field_im, 1, inner, lambda x, y: image_at(x - 1, y - 1), write_second, nz)
+    for x, y in own:
+        base_ref[x, y, 0:cols, :] = split_dot(*alpha_split, *loads_split(x, y), 1, 0)
     if len(plans[2]) > 1:
         wait_units(sum_units(2, 1), sent)
 
@@ -642,7 +708,7 @@
     vmem = pl.BlockSpec(memory_space=pltpu.VMEM)
     anywhere = pl.BlockSpec(memory_space=pl.ANY)
     full = nz + LANES
-    tiles = 2 * ((nz // LANES) * 2 * (nx + ny + 2) + 26) + 8 * (nx * ny * nz // (cols * LANES))
+    tiles = (nz // LANES) * 4 * (nx + ny + 4) + 18 + 8 * (nx * ny * nz // (cols * LANES))
     credits = tiles * TILE_UNITS // cols + 2 * sum(slots(phases) for phases in plans)
     base, pair, coef = pl.pallas_call(
         functools.partial(main_body, sizes, plans, stiffness_values()),
@@ -656,25 +722,24 @@
         scratch_shapes=[
             pltpu.VMEM((nx, ny, 2 * cols, nz), F32),
             pltpu.VMEM((nx, ny, 2 * cols, nz), BF16),
-            pltpu.VMEM((nx + 2, ny + 2, cols, nz), BF16),
-            pltpu.VMEM((nx + 2, ny + 2, cols, nz), BF16),
+            pltpu.VMEM((nx + 4, ny + 4, cols, nz), BF16),
+            pltpu.VMEM((nx, ny, cols, nz), BF16),
             pltpu.VMEM((3, 3, nx * ny, nz), BF16),
-            pltpu.VMEM((2, cols, LANES), BF16),
-            pltpu.VMEM((3, 3, 2, cols, LANES), BF16),
-            pltpu.VMEM((cols, LANES), BF16),
-            pltpu.VMEM((3, 3, cols, LANES), BF16),
+            pltpu.VMEM((2, cols // 2, LANES), BF16),
+            pltpu.VMEM((3, 3, 2, cols // 2, LANES), BF16),
+            pltpu.VMEM((nx + 4, ny + 4, cols, full), F32),
             pltpu.VMEM((nx + 2, ny + 2, cols, full), F32),
-            pltpu.VMEM((nx + 1, ny + 1, 8, full), F32),
-            pltpu.VMEM((nx + 1, ny + 1, 8, full), F32),
-            pltpu.VMEM((nx + 1, ny + 1, 8, full), F32),
-            pltpu.VMEM((3, nx, ny, 8, full), F32),
+            pltpu.VMEM((nx + 3, ny + 3, 8, full), F32),
+            pltpu.VMEM((nx + 3, ny + 3, 8, full), F32),
+            pltpu.VMEM((nx + 3, ny + 3, 8, full), F32),
+            pltpu.VMEM((3, nx + 2, ny + 2, 8, full), F32),
             pltpu.VMEM((slots(plans[0]), cols * cols // LANES, LANES), F32),
             pltpu.VMEM((slots(plans[1]), 2 * cols * cols // LANES, LANES), F32),
             pltpu.VMEM((slots(plans[2]), cols * cols // LANES, LANES), F32),
-            pltpu.VMEM((nx, ny, cols, LANES), F32),
             pltpu.SMEM(moduli.shape, F32),
             pltpu.VMEM(material.shape, jnp.int32),
             pltpu.VMEM((credits, cols * cols // LANES, LANES), F32),
+            pltpu.SemaphoreType.DMA,
             pltpu.SemaphoreType.DMA,
             pltpu.SemaphoreType.DMA((2,)),
             pltpu.SemaphoreType.DMA((sum(len(phases) for phases in plans),)),

time: 20.2 us -> 18.9 us (0.936)
  Pallas kernels: 19.4 us -> 18.1 us
    pallas_call x1, Pallas kernels: 18.4 us -> 17.2 us  [on_device(): pl.pallas_call(functools.partial(main_body, sizes, plans, stiffness_value...]
where the time goes in v4:
time: 18.9 us; the launch traced here: 18.7 us
  Pallas kernels  18.1 us (96%)
  between operations  0.64 us (3%)
    pallas_call x1, Pallas kernels, on_device(): pl.pallas_call(functools.partial(main_body, sizes, plans, stiffness_value...  17.2 us
    pallas_call x1, Pallas kernels, on_device(): pl.pallas_call(last_body, out_shape=(out, out), in_specs=[vmem, vmem, vme...  0.92 us

profile of v4, /device:TPU:0, one launch (start us, length us, event | category | flops | bytes accessed | tf_op | source)
XLA Modules:
  0.0 18.7 jit_solution(14109282679128100198)
XLA Ops:
  0.6 17.2 %shard_map.50 = (f32[2,4,32,256]{3,2,1,0:T(8,128)S(1)}, bf16[2,4,2,32,256]{4,3,2,1,0:T(8,128)(2,1)S(1)}, bf16[32,16]{1,0:T(8,128)(2,1)S(1)}) custom-call(f32[8]{0:T(128)} %moduli_hbm.1, f32[16,2,4,256]{3,2,1,0:T(4,128)} %loads_ref.1, s32[2,4,256]{2,1,0:T(4,128)} %mat_hbm.1), custom_call_target="tpu_custom_call" | custom-call | tf_op jit(solution)/shard_map/pallas_call | solution.py:713
  17.8 0.9 %shard_map.51 = (f32[16,2,4,256]{3,2,1,0:T(4,128)}, f32[16,2,4,256]{3,2,1,0:T(4,128)}) custom-call(bf16[32,16]{1,0:T(8,128)(2,1)S(1)} %get-tuple-element.5.coef_ref, f32[2,4,32,256]{3,2,1,0:T(8,128)S(1)} %get-tuple-element.6.base_ref, bf16[2,4,2,32,256]{4,3,2,1,0:T(8,128)(2,1)S(1)} %get-tuple-element.7.pair_ref), custom_call_target="tpu_custom_call" | custom-call | tf_op jit(solution)/shard_map/pallas_call | solution.py:752

commit v5 on v4

--- a/solution.py
+++ b/solution.py
@@ -117,6 +117,11 @@
     return both[0:rows] + both[rows:] + dot(left_high, right_low, left_dim, right_dim, None)
 
 
+def thirds(value):
+    high, low = halves(value)
+    return high, low, ((value - high.astype(F32)) - low.astype(F32)).astype(BF16)
+
+
 def tree_sum(terms):
     while len(terms) > 1:
         terms = [a + b for a, b in zip(terms[0::2], terms[1::2])] + terms[len(terms) & ~1 :]
@@ -124,24 +129,24 @@
 
 
 def main_body(sizes, plans, stiff, moduli_hbm, loads_ref, mat_hbm, base_ref, pair_ref, coef_ref,
-              stack, low, padded, padded_im, mats_rx, ends, ends_rx, field, field_im, wt, wtr, level, node,
-              shares_square, shares_table, shares_last, moduli_ref, mat_ref, credit,
+              stack, low, third, wide, padded, padded_im, mats_rx, ends, ends_rx, field, field_im, wt, wtr, level, node,
+              shares_square, shares_cross, shares_quad, shares_last, moduli_ref, mat_ref, credit,
               sent, sent_first, halo_recv, sum_recv, local_sems, vouch_sem):
     cols, nx, ny, nz = loads_ref.shape
     mats = moduli_ref.shape[0]
     me = [lax.axis_index(axis) for axis in AXES]
     k_self, k_edge, k_far = stiff[0], stiff[1], stiff[2]
     assert k_edge == 0.0 and stiff[2] == stiff[3]
-    assert 4 * nx * ny <= IDS and (nx * ny * nz) % (cols * LANES) == 0 and nz % LANES == 0 and TILE_UNITS % cols == 0
+    assert 4 * nx * ny <= IDS and nx * ny <= 8 and (nx * ny * nz) % (cols * LANES) == 0 and nz % LANES == 0 and TILE_UNITS % cols == 0
     assert nx >= 2 and ny >= 2
-    shares_of = (shares_square, shares_table, shares_last)
+    shares_of = (shares_square, shares_cross, shares_quad, shares_last)
     own = list(itertools.product(range(nx), range(ny)))
 
     directions = [
         d for d in itertools.product((-1, 0, 1), repeat=3)
         if any(d) and all(step == 0 or sizes[i] > 1 for i, step in enumerate(d))
     ]
-    directions.sort(key=lambda d: -sum(abs(step) for step in d))
+    directions.sort(key=lambda d: (-sum(abs(step) for step in d), d[0] == 0))
 
     def exists(direction):
         good = None
@@ -342,9 +347,9 @@
                 pl.semaphore_wait(vouch_sem.at[round_, 1 if dz > 0 else 0], 1)
 
     lane = lax.broadcasted_iota(jnp.int32, (1, LANES), 1)
-
-    def spread(firsts, lasts, row, first, last, at):
-        spot = at + 4 * row
+    id_spot = IDS + 4 * (nx * ny - 1)
+
+    def spread(firsts, lasts, spot, first, last):
         ahead = jnp.logical_and(lane >= spot, lane < spot + 2)
         start = (spot - 2) % LANES
         behind = jnp.logical_and(lane >= start, lane < start + 2)
@@ -360,13 +365,13 @@
         row = x * ny + y
         first = jnp.broadcast_to(ids[row : row + 1, 0:LANES], (cols, LANES))
         last = jnp.broadcast_to(ids[row : row + 1, nz - LANES : nz], (cols, LANES))
-        firsts, lasts = spread(firsts, lasts, row, first, last, IDS)
+        firsts, lasts = spread(firsts, lasts, id_spot - 4 * row, first, last)
     whole = stack.at[:, :, pl.ds(0, cols), :]
     pltpu.make_async_copy(whole, whole, local_sems.at[0]).wait()
     for x, y in own:
         values = stack[x, y, 0:cols, :]
         padded[x + 2, y + 2] = values.astype(BF16)
-        firsts, lasts = spread(firsts, lasts, x * ny + y, values[:, 0:LANES], values[:, nz - LANES : nz], 0)
+        firsts, lasts = spread(firsts, lasts, 4 * (x * ny + y), values[:, 0:LANES], values[:, nz - LANES : nz])
     upper = cols // 2
     for side, tile in enumerate((firsts, lasts)):
         lower_half = jnp.logical_and(lane >= 2 * LANES // 4 - 2, lane < LANES - 2)
@@ -418,7 +423,7 @@
         return sum(len(phases) for phases in plans[:round_]) + number
 
     def sum_units(round_, number):
-        return (group_of(plans[round_][number])[0] - 1) * (2 if round_ == 1 else 1)
+        return (group_of(plans[round_][number])[0] - 1)
 
     def sum_finish(round_, number):
         total = sum_units(round_, number)
@@ -471,12 +476,10 @@
             for bx, by in itertools.product(range(3), repeat=2)
         }
 
-    def tail_of(tiles, x, y, at=0):
+    def tail_of(tiles, x, y):
         bx, by, row = block_of(x, y)
         tile = tiles[bx, by]
-        near, far = ((2 * LANES - spot - 4 * row) % LANES for spot in (at, at + LANES // 2))
-        if at:
-            return pltpu.roll(tile, near, 1)
+        near, far = ((2 * LANES - spot - 4 * row) % LANES for spot in (0, LANES // 2))
         return jnp.concatenate([pltpu.roll(tile, near, 1), pltpu.roll(tile, far, 1)], axis=0)
 
     def modulus_of(ids):
@@ -492,24 +495,24 @@
     sum_turn(0)
     full = nz + LANES
     tails = merged(ends_rx)
-    flats = {
-        key: own_modulus if key == (1, 1) else modulus_of(mats_rx[key].astype(F32)) for key in tails
-    }
-    sides = {key: modulus_of(tile) for key, tile in tails.items()}
-    moduli = {}
-
-    def modulus_at(x, y):
-        if (x, y) not in moduli:
+    dense = {}
+    for key in tails:
+        flat_ids = own_modulus if key == (1, 1) else modulus_of(mats_rx[key].astype(F32))
+        side = pltpu.roll(modulus_of(tails[key]), LANES - id_spot, 1, stride=4, stride_axis=0)
+        both = jnp.concatenate([flat_ids, side], axis=1)
+        dense[key] = ((0.125 * k_far) * (both + pltpu.roll(both, full - 1, 1)),
+                      (0.125 * k_far) * (both + pltpu.roll(both, 1, 1)))
+    sums = {}
+
+    def sum_at(x, y):
+        if (x, y) not in sums:
             bx, by, row = block_of(x, y)
-            moduli[x, y] = jnp.concatenate([
-                jnp.broadcast_to(flats[bx, by][row : row + 1, :], (8, nz)), tail_of(sides, x, y, IDS)
-            ], axis=1)
-        return moduli[x, y]
+            sums[x, y] = [jnp.broadcast_to(part[row : row + 1, :], (8, full)) for part in dense[bx, by]]
+        return sums[x, y]
 
     def weigh(x, y):
-        total = (modulus_at(x, y) + modulus_at(x, y + 1)) + (modulus_at(x + 1, y) + modulus_at(x + 1, y + 1))
-        total = (0.125 * k_far) * total
-        after, before = total + pltpu.roll(total, full - 1, 1), total + pltpu.roll(total, 1, 1)
+        around = [sum_at(x, y), sum_at(x, y + 1), sum_at(x + 1, y), sum_at(x + 1, y + 1)]
+        after, before = (tree_sum([pair[side] for pair in around]) for side in range(2))
         wt[x, y], wtr[x, y], level[x, y] = after, before, before + after
 
     def around_of(weights, x, y):
@@ -580,7 +583,8 @@
         return jnp.concatenate([padded[x + 2, y + 2], padded_im[x, y]], axis=0), low[x, y]
 
     both_part = gram(image_split, pair_split)
-    sum_start(1, 0, jnp.concatenate([pack(both_part[:, 0:cols]), pack(both_part[:, cols:])], axis=0))
+    sum_start(1, 0, pack(both_part[:, 0:cols]))
+    sum_start(2, 0, pack(both_part[:, cols:]))
     for key in itertools.product(range(nx + 3), range(ny + 3)):
         if key not in near_elements:
             weigh(*key)
@@ -607,37 +611,51 @@
         last_parts.append(split_dot(*image_split(x - 1, y - 1), *halves(image), 1, 1))
 
     operate(field_im, 1, inner, lambda x, y: image_at(x - 1, y - 1), write_last, nz)
-    sum_start(2, 0, pack(tree_sum(last_parts)))
+    sum_start(3, 0, pack(tree_sum(last_parts)))
 
     square = unpack(sum_rest(0), cols)
     sum_turn(1)
+    sum_turn(2)
     row_id = lax.broadcasted_iota(jnp.int32, (cols, LANES), 0)
     col_id = lax.broadcasted_iota(jnp.int32, (cols, LANES), 1)
     eye = jnp.where(row_id == col_id, 1.0, 0.0)
     inverse = solve(columns_of(square), rows_of(eye))
-    table = sum_rest(1)
-    half = table.shape[0] // 2
-    cross, quad = unpack(table[0:half], cols), unpack(table[half:], cols)
+    cells = list(itertools.product(range(nx + 2), range(ny + 2)))
+    for x, y in cells:
+        wide[x, y, 0:cols, :] = field[x + 1, y + 1].astype(BF16)
+        wide[x, y, cols:, :] = field_im[x, y].astype(BF16)
+    for x, y in own:
+        high = jnp.concatenate([padded[x + 2, y + 2], padded_im[x, y]], axis=0).astype(F32)
+        third[x, y] = ((stack[x, y] - high) - low[x, y].astype(F32)).astype(BF16)
+
+    def mixture(parts, cell, rows):
+        x, y = cell
+        if cell not in inner:
+            product = dot(jnp.concatenate(parts[0:2], axis=0), wide[x, y, rows, :], 1, 0, None)
+            return product[0:cols] + product[cols:]
+        one = dot(jnp.concatenate(parts, axis=0), wide[x, y, rows, :], 1, 0, None)
+        two = dot(jnp.concatenate(parts[0:2], axis=0), low[x - 1, y - 1, rows, :], 1, 0, None)
+        three = dot(parts[0], third[x - 1, y - 1, rows, :], 1, 0, None)
+        small = (one[cols : 2 * cols, 0:nz] + two[0:cols]) + ((one[2 * cols :, 0:nz] + two[cols:]) + three)
+        return jnp.concatenate([one[0:cols, 0:nz] + small, one[0:cols, nz:] + one[cols : 2 * cols, nz:]], axis=1)
+
+    cross = unpack(sum_rest(1), cols)
     cross = 0.5 * (cross + turn(cross))
     cross_columns = columns_of(cross)
     alpha_rows = solve(cross_columns, rows_of(square))
     alpha_t = turn(jnp.concatenate(alpha_rows, axis=0))
     alpha_columns = columns_of(alpha_t)
+    quad = unpack(sum_rest(2), cols)
     moved, stood = weave(columns_of(quad), alpha_rows), weave(cross_columns, alpha_rows)
     alpha_t = alpha_t[:, 0:cols]
     alpha_split = halves(alpha_t)
-    alpha_both = jnp.concatenate(alpha_split, axis=0)
-    cells = list(itertools.product(range(nx + 2), range(ny + 2)))
-
-    def start_of(cell):
-        return nz if cell in inner else 0
-
-    for x, y in cells:
-        start = start_of((x, y))
-        twice = dot(alpha_both, field_im[x, y, :, start:].astype(BF16), 1, 0, None)
-        field_im[x, y, :, start:] = field[x + 1, y + 1, :, start:] - (twice[0:cols] + twice[cols:])
-        if (x, y) in inner:
-            base_ref[x - 1, y - 1, cols:, :] = loads_at(x - 1, y - 1) - dot(alpha_t, image_at(x - 1, y - 1), 1, 0)
+    alpha_parts = thirds(alpha_t)
+    for cell in cells:
+        x, y = cell
+        base = field[x + 1, y + 1]
+        if cell in inner:
+            base = jnp.concatenate([loads_at(x - 1, y - 1), base[:, nz:]], axis=1)
+        field_im[x, y] = base - mixture(alpha_parts, cell, slice(cols, 2 * cols))
     updated = square + weave(alpha_columns, rows_of(moved)) - (stood + turn(stood))
     beta_t = weave(columns_of(updated), inverse)
     grown_t = eye + beta_t
@@ -645,27 +663,26 @@
     joint = weave(grown_columns, rows_of(moved))
     known = weave(columns_of(weave(grown_columns, rows_of(cross))), rows_of(turn(grown_t))) - (joint + turn(joint))
     beta_t = beta_t[:, 0:cols]
-    beta_both = jnp.concatenate(halves(beta_t), axis=0)
-    for x, y in cells:
-        start = start_of((x, y))
-        twice = dot(beta_both, field[x + 1, y + 1, :, start:].astype(BF16), 1, 0, None)
-        mixed = field_im[x, y, :, start:] + (twice[0:cols] + twice[cols:])
-        if (x, y) in inner:
-            direction = base_ref[x - 1, y - 1, cols:, :] + dot(beta_t, loads_at(x - 1, y - 1), 1, 0)
-            mixed = jnp.concatenate([direction, mixed], axis=1)
-        rounded = mixed.astype(BF16)
+    beta_parts = thirds(beta_t)
+    for cell in cells:
+        x, y = cell
+        rest = field_im[x, y]
+        direction = rest + mixture(beta_parts, cell, slice(0, cols))
+        rounded = direction.astype(BF16)
         field_im[x, y] = rounded.astype(F32)
-        if (x, y) in inner:
+        if cell in inner:
+            base_ref[x - 1, y - 1, cols:, :] = rest[:, 0:nz]
+            direction, rounded = direction[:, 0:nz], rounded[:, 0:nz]
             stack[x - 1, y - 1, cols:, :] = direction
-            pair_ref[x - 1, y - 1, 0, 0:cols, :] = rounded[:, 0:nz]
-            pair_ref[x - 1, y - 1, 0, cols:, :] = (direction - rounded[:, 0:nz].astype(F32)).astype(BF16)
+            pair_ref[x - 1, y - 1, 0, 0:cols, :] = rounded
+            pair_ref[x - 1, y - 1, 0, cols:, :] = (direction - rounded.astype(F32)).astype(BF16)
 
     halo_wait((1,), sent, sum(
-        sum_units(round_, number) for round_ in range(3) for number in range(len(plans[round_]))
-        if (round_, number) != (2, 1)
+        sum_units(round_, number) for round_ in range(4) for number in range(len(plans[round_]))
+        if (round_, number) != (3, 1)
     ))
-    sum_turn(2)
-    last = unpack(sum_rest(2), cols)
+    sum_turn(3)
+    last = unpack(sum_rest(3), cols)
     total = known + weave(alpha_columns, rows_of(weave(columns_of(last), alpha_rows)))
     last_rows = solve(columns_of(total), rows_of(updated))
     coef_t = jnp.concatenate(last_rows, axis=0)[:, 0:cols].T
@@ -677,8 +694,8 @@
     operate(field_im, 1, inner, lambda x, y: image_at(x - 1, y - 1), write_second, nz)
     for x, y in own:
         base_ref[x, y, 0:cols, :] = split_dot(*alpha_split, *loads_split(x, y), 1, 0)
-    if len(plans[2]) > 1:
-        wait_units(sum_units(2, 1), sent)
+    if len(plans[3]) > 1:
+        wait_units(sum_units(3, 1), sent)
 
 
 def last_body(coef_ref, base_ref, pair_ref, sol_ref, res_ref, stage, sems):
@@ -700,7 +717,7 @@
     count = int(np.prod(sizes))
     split = (("gx", "gy"), ("gz",))
     quick = (AXES,) if count <= DIRECT_LIMIT else split
-    plans = (split, quick, quick)
+    plans = (split, quick, quick, quick)
 
     def slots(phases):
         return sum(int(np.prod([sizes[AXES.index(a)] for a in axes])) for axes in phases)
@@ -722,6 +739,8 @@
         scratch_shapes=[
             pltpu.VMEM((nx, ny, 2 * cols, nz), F32),
             pltpu.VMEM((nx, ny, 2 * cols, nz), BF16),
+            pltpu.VMEM((nx, ny, 2 * cols, nz), BF16),
+            pltpu.VMEM((nx + 2, ny + 2, 2 * cols, full), BF16),
             pltpu.VMEM((nx + 4, ny + 4, cols, nz), BF16),
             pltpu.VMEM((nx, ny, cols, nz), BF16),
             pltpu.VMEM((3, 3, nx * ny, nz), BF16),
@@ -734,8 +753,9 @@
             pltpu.VMEM((nx + 3, ny + 3, 8, full), F32),
             pltpu.VMEM((3, nx + 2, ny + 2, 8, full), F32),
             pltpu.VMEM((slots(plans[0]), cols * cols // LANES, LANES), F32),
-            pltpu.VMEM((slots(plans[1]), 2 * cols * cols // LANES, LANES), F32),
+            pltpu.VMEM((slots(plans[1]), cols * cols // LANES, LANES), F32),
             pltpu.VMEM((slots(plans[2]), cols * cols // LANES, LANES), F32),
+            pltpu.VMEM((slots(plans[3]), cols * cols // LANES, LANES), F32),
             pltpu.SMEM(moduli.shape, F32),
             pltpu.VMEM(material.shape, jnp.int32),
             pltpu.VMEM((credits, cols * cols // LANES, LANES), F32),

time: 18.9 us -> 18.8 us (level)
  no operation moved by 1% of the time
where the time goes in v5:
time: 18.8 us; the launch traced here: 18.7 us
  Pallas kernels  18 us (96%)
  between operations  0.64 us (3%)
    pallas_call x1, Pallas kernels, on_device(): pl.pallas_call(functools.partial(main_body, sizes, plans, stiffness_value...  17.1 us
    pallas_call x1, Pallas kernels, on_device(): pl.pallas_call(last_body, out_shape=(out, out), in_specs=[vmem, vmem, vme...  0.92 us

profile of v5, /device:TPU:0, one launch (start us, length us, event | category | flops | bytes accessed | tf_op | source)
XLA Modules:
  0.0 18.7 jit_solution(11604312853839010135)
XLA Ops:
  0.6 17.1 %shard_map.50 = (f32[2,4,32,256]{3,2,1,0:T(8,128)S(1)}, bf16[2,4,2,32,256]{4,3,2,1,0:T(8,128)(2,1)S(1)}, bf16[32,16]{1,0:T(8,128)(2,1)S(1)}) custom-call(f32[8]{0:T(128)} %moduli_hbm.1, f32[16,2,4,256]{3,2,1,0:T(4,128)} %loads_ref.1, s32[2,4,256]{2,1,0:T(4,128)} %mat_hbm.1), custom_call_target="tpu_custom_call" | custom-call | tf_op jit(solution)/shard_map/pallas_call | solution.py:730
  17.7 0.9 %shard_map.51 = (f32[16,2,4,256]{3,2,1,0:T(4,128)}, f32[16,2,4,256]{3,2,1,0:T(4,128)}) custom-call(bf16[32,16]{1,0:T(8,128)(2,1)S(1)} %get-tuple-element.5.coef_ref, f32[2,4,32,256]{3,2,1,0:T(8,128)S(1)} %get-tuple-element.6.base_ref, bf16[2,4,2,32,256]{4,3,2,1,0:T(8,128)(2,1)S(1)} %get-tuple-element.7.pair_ref), custom_call_target="tpu_custom_call" | custom-call | tf_op jit(solution)/shard_map/pallas_call | solution.py:772

commit v6 on v5

--- a/solution.py
+++ b/solution.py
@@ -456,11 +456,11 @@
 
     square_part = gram(loads_split, loads_split)
     sum_start(0, 0, pack(square_part))
+    halo_wait((0,), sent_first)
+    halo_start(1)
     for round_ in range(1, vouches):
         vouched(round_ - 1)
         vouch(round_)
-    halo_wait((0,), sent_first)
-    halo_start(1)
     moduli_copy.wait()
 
     def block_of(x, y):

time: 18.8 us -> 18.8 us (level)
  no operation moved by 1% of the time
where the time goes in v6:
time: 18.8 us; the launch traced here: 18.7 us
  Pallas kernels  18 us (96%)
  between operations  0.64 us (3%)
    pallas_call x1, Pallas kernels, on_device(): pl.pallas_call(functools.partial(main_body, sizes, plans, stiffness_value...  17.1 us
    pallas_call x1, Pallas kernels, on_device(): pl.pallas_call(last_body, out_shape=(out, out), in_specs=[vmem, vmem, vme...  0.92 us

profile of v6, /device:TPU:0, one launch (start us, length us, event | category | flops | bytes accessed | tf_op | source)
XLA Modules:
  0.0 18.7 jit_solution(15619507686927231929)
XLA Ops:
  0.6 17.1 %shard_map.50 = (f32[2,4,32,256]{3,2,1,0:T(8,128)S(1)}, bf16[2,4,2,32,256]{4,3,2,1,0:T(8,128)(2,1)S(1)}, bf16[32,16]{1,0:T(8,128)(2,1)S(1)}) custom-call(f32[8]{0:T(128)} %moduli_hbm.1, f32[16,2,4,256]{3,2,1,0:T(4,128)} %loads_ref.1, s32[2,4,256]{2,1,0:T(4,128)} %mat_hbm.1), custom_call_target="tpu_custom_call" | custom-call | tf_op jit(solution)/shard_map/pallas_call | solution.py:730
  17.7 0.9 %shard_map.51 = (f32[16,2,4,256]{3,2,1,0:T(4,128)}, f32[16,2,4,256]{3,2,1,0:T(4,128)}) custom-call(bf16[32,16]{1,0:T(8,128)(2,1)S(1)} %get-tuple-element.5.coef_ref, f32[2,4,32,256]{3,2,1,0:T(8,128)S(1)} %get-tuple-element.6.base_ref, bf16[2,4,2,32,256]{4,3,2,1,0:T(8,128)(2,1)S(1)} %get-tuple-element.7.pair_ref), custom_call_target="tpu_custom_call" | custom-call | tf_op jit(solution)/shard_map/pallas_call | solution.py:772
